TPU v7x, 32 devices: a whole 2x2x4 slice. The times are simulated.
32 devices in a mesh: pair: 8 (over y, x, core), tm: 4 (over z).
Axes of the slice: x: 2, y: 2, z: 4, core: 2. Of those that a mesh axis runs over, the one named last changes fastest.
Arguments:
- three_centre: bfloat16 [1536, 16384], P(None, 'pair'), may hold values from -0.09375 to 0.09375
- root_coulomb: bfloat16 [1536, 1536], P(('pair', 'tm')), may hold values from -0.15625 to 0.15625
- occ_depth: float32 [256], replicated, may hold values from 0.1 to 1
- vir_energy: float32 [1024], replicated, may hold values from 0.01 to 500
- occ_block: int32 [64], P('pair'), may hold values from 0 to 15
- vir_block: int32 [64], P('pair'), may hold values from 0 to 63
Outputs:
- screened: float32 [4, 1536, 1536], P('tm', 'pair')
All inputs are finite; a program needn't handle non-finite values.
Results may differ from a plain program's by a relative error of at most 0.003.
Values may be sent and summed in bfloat16 or wider, within the bound.
No kernel may reach another device: no remote copies, remote signals or barrier semaphores. Data moves between devices by JAX's collectives and lax.ppermute only.
A program may use at most 128 MiB of HBM per device.

v0:
```python
import math

import jax
import jax.numpy as jnp
from jax import lax
from jax.sharding import PartitionSpec as P

OB = 16
VB = 16
NOB = 16
NVB = 64
TIME_DEV = 1


log_span = math.log(5000.0)


def shards(three_centre, root_coulomb, occ_depth, vir_energy, occ_block, vir_block):
    n_pair = lax.axis_size("pair")
    n_times = lax.axis_size("tm") * TIME_DEV
    naux = three_centre.shape[0]
    rows = naux // n_pair
    occ_table = occ_depth.reshape(NOB, OB)
    vir_table = vir_energy.reshape(NVB, VB)
    occ_onehot = (occ_block[:, None] == jnp.arange(NOB, dtype=jnp.int32)[None, :]).astype(
        jnp.float32
    )
    vir_onehot = (vir_block[:, None] == jnp.arange(NVB, dtype=jnp.int32)[None, :]).astype(
        jnp.float32
    )
    occ_sel = jnp.dot(occ_onehot, occ_table, precision=lax.Precision.HIGHEST)
    vir_sel = jnp.dot(vir_onehot, vir_table, precision=lax.Precision.HIGHEST)
    gap = (occ_sel[:, :, None] + vir_sel[:, None, :]).reshape(-1)
    steps_t = jnp.arange(n_times).astype(jnp.float32)
    taus = 0.002 * jnp.exp(steps_t * (log_span / max(n_times - 1, 1)))
    omegas = (steps_t + 0.5) / n_times
    coef = 2.4 * omegas[:, None] * jnp.cos(jnp.pi * omegas[:, None] * (steps_t[None, :] + 0.5))
    first_freq = lax.axis_index("tm") * TIME_DEV
    my_coef = lax.dynamic_slice_in_dim(coef, first_freq, TIME_DEV, 0)
    decays = jnp.exp(-gap[None, :] * taus[:, None])
    weights = jnp.dot(my_coef, decays, precision=lax.Precision.HIGHEST)
    weighted = (three_centre.astype(jnp.float32) * weights[0][None, :]).astype(jnp.bfloat16)
    blocks = lax.dot_general(
        weighted, three_centre, (((1,), (1,)), ((), ())), preferred_element_type=jnp.float32
    )
    chi_flat = lax.psum_scatter(blocks, "pair", scatter_dimension=0, tiled=True)
    chi_low = chi_flat.reshape(rows, TIME_DEV, naux).transpose(1, 0, 2).astype(jnp.bfloat16)
    return jnp.einsum(
        "frc,cd->frd",
        chi_low,
        lax.all_gather(root_coulomb, ("pair", "tm"), axis=0, tiled=True),
        preferred_element_type=jnp.float32,
    )


def solution(mesh):
    in_specs = (P(None, "pair"), P(("pair", "tm"), None), P(), P(), P("pair"), P("pair"))
    out_specs = P("tm", "pair", None)
    return jax.shard_map(shards, mesh=mesh, in_specs=in_specs, out_specs=out_specs, check_vma=False)
```

profile of v0, /device:TPU:0, one launch (start us, length us, event | category | flops | bytes accessed | tf_op | source)
XLA Modules:
  0.0 128.1 jit_solution(10082277118126008667)
XLA Ops:
  7.4 0.0 all-gather.2.cloned.1.call-start
  7.4 0.7 all-gather.2.cloned.1.call-update
  8.1 0.0 reduce-scatter.2.cloned.1.call-start
  8.1 0.8 reshape.59
  8.9 0.8 reshape.58
  9.7 0.8 fusion.8
  10.5 0.8 fusion.9
  11.3 0.1 add_negate_fusion
  11.4 0.1 neg.12
  11.6 0.1 cosine_multiply_fusion
  11.7 0.3 fusion.3
  11.9 15.9 %fusion = f32[1536,1536]{1,0:T(8,128)} fusion(bf16[1536,2048]{1,0:T(8,128)(2,1)} %param.6, f32[2048]{0:T(1024)S(1)} %bitcast.11), kind=kOutput, calls=%fused_computation.1 | convolution fusion | flops 9673113600 | bytes 15736832 | tf_op jit(solution)/shard_map/dot_general | solution.py:43
  27.9 0.0 reduce-scatter.2.cloned.1.call-update
  27.9 61.4 %all-gather.2.cloned.1.call-done = bf16[1536,1536]{1,0:T(8,128)(2,1)} async-done(((bf16[48,1536]{1,0:T(8,128)(2,1)}), bf16[1536,1536]{1,0:T(8,128)(2,1)}) %all-gather.2.cloned.1.call-update) | async-done | bytes 4718608 | tf_op jit(solution)/shard_map/all_gather | solution.py:51
  89.3 26.5 %reduce-scatter.2.cloned.1.call-done = f32[192,1536]{1,0:T(8,128)} async-done(((f32[1536,1536]{1,0:T(8,128)}), f32[192,1536]{1,0:T(8,128)}) %reduce-scatter.2.cloned.1.call-update) | async-done | bytes 1179664 | tf_op jit(solution)/shard_map/reduce_scatter | solution.py:46
  115.8 4.8 %convolution_bitcast_fusion = f32[1,192,1536]{2,1,0:T(8,128)} fusion(bf16[1536,1536]{1,0:T(8,128)(2,1)} %all-gather.2.cloned.1.call-done, f32[192,1536]{1,0:T(8,128)} %reduce-scatter.2.cloned.1.call-done), kind=kOutput, calls=%fused_computation.3 | convolution fusion | flops 906264576 | bytes 7077888 | tf_op jit(solution)/shard_map/frc,cd->frd/dot_general | solution.py:48
  (3 shorter events, 0.0 us)
Async XLA Ops:
  7.4 82.0 %all-gather.2.cloned.1.call-start = ((), (), s32[]{:S(2)}) async-start(), calls=%async_computation.2 | async-start | bytes 4866048 | tf_op jit(solution)/shard_map/all_gather | solution.py:51
  8.1 107.7 %reduce-scatter.2.cloned.1.call-start = ((), (), s32[]{:S(2)}) async-start(), calls=%async_computation.1 | async-start | bytes 10616832 | tf_op jit(solution)/shard_map/reduce_scatter | solution.py:46
Sparse Core Ops, SparseCore 0:
  11.0 78.3 all-gather.1
Sparse Core Ops, SparseCore 1:
  28.0 87.8 reduce-scatter.1
where the time goes:
time: 128 us
  waiting for transfers between devices  88.6 us (69%)
  matrix products  22.7 us (18%)
  between operations  14.9 us (12%)
  local copies, waits for them, and re-layouts  1.6 us (1%)
    all_gather x1, waiting for transfers between devices, shards(): lax.all_gather(root_coulomb, ('pair', 'tm'), axis=0, tiled=True)  61.4 us
    reduce_scatter x1, waiting for transfers between devices, shards(): chi_flat = lax.psum_scatter(blocks, 'pair', scatter_dimension=0, tiled=True)  26.5 us
    dot_general x1, matrix products, shards(): lax.dot_general(weighted, three_centre, (((1,), (1,)), ((), ())), preferr...  15.9 us
    dot_general x1, matrix products, shards(): jnp.einsum('frc,cd->frd', chi_low, lax.all_gather(root_coulomb, ('pair',...  4.8 us
  transfers between devices with their start and end apart: 2, of which 2 were waited for; matrix products, arithmetic and copies ran while one was open for 15% of the time, Pallas kernels for 0%

commit v1 on v0

v1 whole, which is shorter than its diff:
```python
import functools
import math

import numpy as np

import jax
import jax.numpy as jnp
from jax import lax
from jax.experimental import pallas as pl
from jax.experimental.pallas import tpu as pltpu
from jax.sharding import PartitionSpec as P


OB = 16
VB = 16
LANES = 128
SUBLANES = 16
TILE = 512
SPLIT = 512


AXES = ("pair", "tm")
LOG_SPAN = math.log(5000.0)


def popcount(mask):
    return bin(mask).count("1")


def time_tables(n_times):
    steps = np.arange(n_times).astype(np.float32)
    taus = (0.002 * np.exp(steps * np.float32(LOG_SPAN / max(n_times - 1, 1)))).astype(np.float32)
    omegas = ((steps + 0.5) / n_times).astype(np.float32)
    angle = np.float32(np.pi) * omegas[:, None] * (steps[None, :] + np.float32(0.5))
    coef = (np.float32(2.4) * omegas[:, None] * np.cos(angle)).astype(np.float32)
    return [float(t) for t in taus], [[float(c) for c in row] for row in coef]


def weights_kernel(taus, coef, occ_block, vir_block, occ_ref, vir_ref, w_ref):
    n_blocks = w_ref.shape[0]
    shape = (n_blocks, LANES)
    row = lax.broadcasted_iota(jnp.int32, shape, 0)
    lane = lax.broadcasted_iota(jnp.int32, shape, 1)

    def table_rows(block_ref, table_ref, width):
        chosen = jnp.zeros(shape, jnp.int32)
        for k in range(n_blocks):
            chosen = jnp.where(row == k, block_ref[k], chosen)
        per_group = LANES // width
        found = jnp.zeros(shape, jnp.float32)
        for group in range(table_ref.shape[1] // LANES):
            part = table_ref[:, group * LANES : (group + 1) * LANES]
            found += jnp.where(lane // width + group * per_group == chosen, part, 0.0)
        shift = width
        while shift < LANES:
            found += pltpu.roll(found, shift, 1)
            shift *= 2
        return found

    occ = table_rows(occ_block, occ_ref, OB)
    vir = table_rows(vir_block, vir_ref, VB)
    mine = lax.axis_index("tm")
    n_times = len(taus)
    for part in range(OB * VB // LANES):
        level = jnp.take_along_axis(occ, lane // VB + part * (LANES // VB), axis=1)
        gap = level + vir
        total = jnp.zeros(shape, jnp.float32)
        for i in range(n_times):
            factor = jnp.float32(0.0)
            for j in range(n_times):
                factor = jnp.where(mine == j, jnp.float32(coef[j][i]), factor)
            total += factor * jnp.exp(-gap * taus[i])
        w_ref[:, part * LANES : (part + 1) * LANES] = total


def scale_rows(scaled, new, source, w_ref):
    width = w_ref.shape[1]
    for k in range(w_ref.shape[0]):
        cols = pl.ds(k * width, width)
        scaled[new, cols] = (source(cols).astype(jnp.float32) * w_ref[k : k + 1, :]).astype(jnp.bfloat16)


def multiply(scaled, right, here, outs, arrived=None):
    total = lax.dot_general(scaled[...], right, (((1,), (1,)), ((), ())), preferred_element_type=jnp.float32)
    rows = outs[0].shape[0]
    for b, out in enumerate(outs):
        value = total[b * rows : (b + 1) * rows]
        if arrived:
            value += arrived[b][:, here].astype(jnp.float32)
        out[:, here] = value.astype(out.dtype)


def blocks_of(layers, n_pair, naux, z):
    if layers == 1:
        return [(0, 0, naux)]
    height = naux // (layers * n_pair)
    return [
        ((p * layers + jnp.bitwise_xor(z, layer)) * height, (layer * n_pair + p) * height, height)
        for layer in range(layers)
        for p in range(n_pair)
    ]


def first_kernel(taus, coef, layers, masks, occ_block, vir_block, occ, vir, source, *refs):
    count = len(masks)
    w_ref, held, outs = refs[0], refs[1], refs[2 : 2 + count]
    occ_b, vir_b, occ_t, vir_t, left, scaled, sems = refs[2 + count :]
    naux, rows = held.shape[0], outs[0].shape[0]
    me, z, n_pair = lax.axis_index("pair"), lax.axis_index("tm"), lax.axis_size("pair")
    small = ((occ_block, occ_b), (vir_block, vir_b), (occ, occ_t), (vir, vir_t))
    pairs = list(small)
    for b, mask in enumerate(masks):
        first = pl.multiple_of(jnp.bitwise_xor(me, mask) * rows, SUBLANES)
        pairs.append((source.at[pl.ds(first, rows), :], left.at[pl.ds(b * rows, rows), :]))
    blocks = blocks_of(layers, n_pair, naux, z)
    for old, new, length in blocks:
        pairs.append((source.at[pl.ds(pl.multiple_of(old, SUBLANES), length), :], held.at[pl.ds(new, length), :]))
    copies = [pltpu.make_async_copy(here, there, sems.at[i]) for i, (here, there) in enumerate(pairs)]
    for copy in copies:
        copy.start()
    for copy in copies[: len(small)]:
        copy.wait()
    weights_kernel(taus, coef, occ_b, vir_b, occ_t, vir_t, w_ref)
    for b in range(count):
        copies[len(small) + b].wait()
        here = pl.ds(b * rows, rows)
        scale_rows(scaled, here, lambda cols: left[here, cols], w_ref)
    waiting = list(zip(copies[len(small) + count :], blocks))
    tile = math.gcd(naux, TILE)
    for n in range(naux // tile):
        while waiting and waiting[0][1][1] < (n + 1) * tile:
            waiting.pop(0)[0].wait()
        here = pl.ds(n * tile, tile)
        multiply(scaled, held[here, :], here, outs)


def first_rows(three_centre, occ_depth, vir_energy, occ_block, vir_block, masks, rows, layers, n_times):
    taus, coef = time_tables(n_times)
    naux, depth = three_centre.shape
    count = len(masks)
    vmem = pl.BlockSpec(memory_space=pltpu.VMEM)
    operands = (occ_block, vir_block, occ_depth.reshape(1, -1), vir_energy.reshape(1, -1), three_centre)
    n_copies = 4 + count + (1 if layers == 1 else layers * lax.axis_size("pair"))
    results = pl.pallas_call(
        functools.partial(first_kernel, taus, coef, layers, masks),
        out_shape=[
            pltpu.VMEM((occ_block.shape[0], OB * VB), jnp.float32),
            pltpu.VMEM(three_centre.shape, three_centre.dtype),
        ]
        + [jax.ShapeDtypeStruct((rows, naux), jnp.bfloat16)] * count,
        in_specs=[pl.BlockSpec(memory_space=pltpu.HBM)] * len(operands),
        out_specs=[vmem] * (2 + count),
        scratch_shapes=[pltpu.SMEM(occ_block.shape, jnp.int32), pltpu.SMEM(vir_block.shape, jnp.int32)]
        + [pltpu.VMEM(v.shape, jnp.float32) for v in operands[2:4]]
        + [pltpu.VMEM((count * rows, depth), jnp.bfloat16)] * 2
        + [pltpu.SemaphoreType.DMA((n_copies,))],
        name="first",
        compiler_params=pltpu.CompilerParams(vmem_limit_bytes=24 * 2**20),
        cost_estimate=pl.CostEstimate(
            flops=2 * count * rows * naux * depth, bytes_accessed=2 * three_centre.size, transcendentals=10**4
        ),
    )(*[pltpu.with_memory_space_constraint(v, pltpu.HBM) for v in operands])
    return results[0], results[1], results[2:]


def partial_kernel(masks, received, layers, w_ref, held, *refs):
    count = len(masks)
    arrived = refs[: count if received else 0]
    outs, scaled = refs[-1 - count : -1], refs[-1]
    rows, naux = outs[0].shape
    me, z, n_pair = lax.axis_index("pair"), lax.axis_index("tm"), lax.axis_size("pair")
    height = rows // layers
    for b, mask in enumerate(masks):
        owner = jnp.bitwise_xor(me, mask)
        for part in range(layers):
            row = owner if layers == 1 else jnp.bitwise_xor(z, part) * n_pair + owner
            old = pl.ds(pl.multiple_of(row * height, SUBLANES), height)
            scale_rows(scaled, pl.ds(b * rows + part * height, height), lambda cols: held[old, cols], w_ref)
    tile = math.gcd(naux, TILE)
    for n in range(naux // tile):
        here = pl.ds(n * tile, tile)
        multiply(scaled, held[here, :], here, outs, arrived)


def partial_rows(held, weights, masks, dtypes, rows, layers, arrived=None):
    naux, depth = held.shape
    count = len(masks)
    vmem = pl.BlockSpec(memory_space=pltpu.VMEM)
    operands = [weights, held] + (arrived or [])
    return pl.pallas_call(
        functools.partial(partial_kernel, masks, arrived is not None, layers),
        in_specs=[vmem] * len(operands),
        out_specs=[vmem] * count,
        scratch_shapes=[pltpu.VMEM((count * rows, depth), jnp.bfloat16)],
        out_shape=[jax.ShapeDtypeStruct((rows, naux), t) for t in dtypes],
        name="partial",
        compiler_params=pltpu.CompilerParams(vmem_limit_bytes=16 * 2**20),
        cost_estimate=pl.CostEstimate(
            flops=2 * count * rows * naux * depth,
            bytes_accessed=2 * (naux + count * rows) * depth + 4 * count * rows * naux,
            transcendentals=0,
        ),
    )(*[pltpu.with_memory_space_constraint(v, pltpu.VMEM) for v in operands[:2]], *operands[2:])


def lay(root, first_layer, last_layer, plan, pieces, height):
    me, z, n_pair = lax.axis_index("pair"), lax.axis_index("tm"), lax.axis_size("pair")
    for piece, (column, needed, blocks) in zip(pieces, plan):
        cols = pl.ds(column, piece.shape[1])

        def move():
            for i, (mask, layer) in enumerate(blocks):
                if first_layer <= layer < last_layer:
                    target = (jnp.bitwise_xor(me, mask) + (layer - first_layer) * n_pair) * height
                    root[pl.ds(pl.multiple_of(target, SUBLANES), height), cols] = piece[i * height : (i + 1) * height, :]

        if needed is None:
            move()
        else:
            pl.when(needed(z))(move)


def choose(pieces, first_layer, last_layer):
    kept = [p for p in pieces if any(first_layer <= layer < last_layer for _, layer in p[2])]
    return [p[:3] for p in kept], [p[3] for p in kept]


def collect_kernel(plan, last_layer, height, *refs):
    lay(refs[-1], 0, last_layer, plan, refs[:-1], height)


def collect(pieces, last_layer, height, naux):
    plan, values = choose(pieces, 0, last_layer)
    rows = last_layer * lax.axis_size("pair") * height
    vmem = pl.BlockSpec(memory_space=pltpu.VMEM)
    return pl.pallas_call(
        functools.partial(collect_kernel, plan, last_layer, height),
        in_specs=[vmem] * len(values),
        out_specs=vmem,
        out_shape=pltpu.VMEM((rows, naux), values[0].dtype),
        name="collect",
        compiler_params=pltpu.CompilerParams(vmem_limit_bytes=8 * 2**20),
        cost_estimate=pl.CostEstimate(flops=10**9, bytes_accessed=4 * rows * naux, transcendentals=0),
    )(*values)


def screen_kernel(n_terms, *refs):
    terms = refs[:n_terms]
    root, out, chi = refs[n_terms:]
    value = terms[0][...].astype(jnp.float32)
    for term in terms[1:]:
        value += term[...].astype(jnp.float32)
    chi[...] = value.astype(jnp.bfloat16)
    tile = math.gcd(out.shape[1], TILE)
    for n in range(out.shape[1] // tile):
        cols = pl.ds(n * tile, tile)
        out[:, cols] = jnp.dot(chi[:, : root.shape[0]], root[:, cols], preferred_element_type=jnp.float32)


def screen(terms, root):
    rows, naux = terms[0].shape
    vmem = pl.BlockSpec(memory_space=pltpu.VMEM)
    return pl.pallas_call(
        functools.partial(screen_kernel, len(terms)),
        in_specs=[vmem] * (len(terms) + 1),
        out_specs=[vmem] * 2,
        out_shape=[
            jax.ShapeDtypeStruct((rows, root.shape[1]), jnp.float32),
            jax.ShapeDtypeStruct((rows, naux), jnp.bfloat16),
        ],
        name="screen",
        compiler_params=pltpu.CompilerParams(vmem_limit_bytes=8 * 2**20),
        cost_estimate=pl.CostEstimate(
            flops=2 * rows * root.size, bytes_accessed=2 * root.size + 6 * rows * naux, transcendentals=0
        ),
    )(*terms, root)


def finish_kernel(plan, layer, height, total, chi, *refs):
    pieces, (out, root, staged, sems) = refs[: len(plan)], refs[len(plan) :]
    lay(root, layer, layer + 1, plan, pieces, height)
    depth = root.shape[0]
    tile = math.gcd(out.shape[2], TILE)
    copies = []
    for n in range(out.shape[2] // tile):
        cols = pl.ds(n * tile, tile)
        staged[:, cols] = total[:, cols] + jnp.dot(
            chi[:, chi.shape[1] - depth :], root[:, cols], preferred_element_type=jnp.float32
        )
        copies.append(pltpu.make_async_copy(staged.at[:, cols], out.at[0, :, cols], sems.at[n]))
        copies[-1].start()
    for copy in copies:
        copy.wait()


def finish(total, chi, pieces, layer, height):
    rows, naux = total.shape
    plan, values = choose(pieces, layer, layer + 1)
    depth = lax.axis_size("pair") * height
    vmem = pl.BlockSpec(memory_space=pltpu.VMEM)
    return pl.pallas_call(
        functools.partial(finish_kernel, plan, layer, height),
        in_specs=[vmem] * (2 + len(values)),
        out_specs=pl.BlockSpec(memory_space=pltpu.HBM),
        out_shape=jax.ShapeDtypeStruct((1, rows, naux), jnp.float32),
        scratch_shapes=[
            pltpu.VMEM((depth, naux), jnp.bfloat16),
            pltpu.VMEM((rows, naux), jnp.float32),
            pltpu.SemaphoreType.DMA((naux // math.gcd(naux, TILE),)),
        ],
        name="finish",
        compiler_params=pltpu.CompilerParams(vmem_limit_bytes=8 * 2**20),
        cost_estimate=pl.CostEstimate(
            flops=2 * rows * depth * naux, bytes_accessed=2 * depth * naux + 8 * rows * naux, transcendentals=0
        ),
    )(total, chi, *values)


def swap(value, mask):
    n_pair = lax.axis_size("pair")
    return lax.ppermute(value, "pair", [(p, p ^ mask) for p in range(n_pair)])


def along(value, moves):
    return lax.ppermute(value, "tm", moves)


def is_inner(z):
    return jnp.logical_or(z == 1, z == 2)


def is_outer(z):
    return jnp.logical_or(z == 0, z == 3)


def gather_root(root_coulomb):
    n_pair, n_tm = lax.axis_size("pair"), lax.axis_size("tm")
    masks = [2 * m for m in range(n_pair // 2)]
    near = [root_coulomb] + [swap(root_coulomb, m) for m in masks[1:]]
    plane = jnp.concatenate([rows[:, SPLIT:] for rows in near], axis=0)
    middle, outward = [(1, 2), (2, 1)], [(1, 0), (2, 3)]
    first = along(plane, [(z, z ^ 1) for z in range(n_tm)])
    second = along(plane, middle)
    inner = along(first, middle)
    outer = along(second, outward)
    last = along(inner, outward)
    pieces = []

    def both(column, needed, blocks, value):
        pieces.append((column, needed, blocks, value))
        pieces.append((column, needed, [(m ^ 1, layer) for m, layer in blocks], swap(value, 1)))

    for value, layer, needed in (
        (plane, 0, None),
        (first, 1, None),
        (second, 3, is_inner),
        (inner, 2, is_inner),
        (outer, 2, is_outer),
        (last, 3, is_outer),
    ):
        both(SPLIT, needed, [(m, layer) for m in masks], value)
    if SPLIT:
        tall = root_coulomb[:, :SPLIT]
        layers = range(n_tm)
        far = [tall] + [along(tall, [(z, z ^ m) for z in layers]) for m in layers[1:]]
        tower = jnp.concatenate(far, axis=0)
        for mask in masks:
            value = swap(tower, mask) if mask else tower
            both(0, None, [(mask, layer) for layer in layers], value)
    return pieces


def shards(layers, three_centre, root_coulomb, occ_depth, vir_energy, occ_block, vir_block):
    n_pair, n_tm = lax.axis_size("pair"), lax.axis_size("tm")
    height = root_coulomb.shape[0]
    rows = three_centre.shape[0] // n_pair
    if layers == 1:
        root = lax.all_gather(root_coulomb, AXES, axis=0, tiled=True)
    else:
        pieces = gather_root(root_coulomb)
        root = collect(pieces, layers - 1, height, three_centre.shape[0])
    halves = []
    groups = chip_groups(n_pair, rows)
    for g, group in enumerate(groups):
        masks = [2 * m + 1 for m in group]
        if g == 0:
            weights, held, parts = first_rows(
                three_centre, occ_depth, vir_energy, occ_block, vir_block, masks, rows, layers, n_tm
            )
        else:
            parts = partial_rows(held, weights, masks, [jnp.bfloat16] * len(group), rows, layers)
        halves.append([swap(part, 1) for part in parts])
    terms = []
    for g, group in enumerate(groups):
        dtypes = [jnp.bfloat16 if m else jnp.float32 for m in group]
        sums = partial_rows(held, weights, [2 * m for m in group], dtypes, rows, layers, halves[g])
        terms += [swap(part, 2 * m) if m else part for m, part in zip(group, sums)]
    total, chi = screen(terms, root)
    if layers == 1:
        return total[None]
    return finish(total, chi, pieces, layers - 1, height)


def chip_groups(n_pair, rows):
    chips = sorted(range(n_pair // 2), key=lambda m: -popcount(m))
    size = max(1, min(len(chips), 384 // rows))
    return [chips[i : i + size] for i in range(0, len(chips), size)]


def solution(mesh):
    n_pair, n_tm = mesh.shape["pair"], mesh.shape["tm"]
    in_specs = (P(None, "pair"), P(("pair", "tm"), None), P(), P(), P("pair"), P("pair"))
    out_specs = P("tm", "pair", None)

    def step(*args):
        height = args[1].shape[0] // (n_pair * n_tm)
        line = n_tm == 4 and n_pair == 8 and height % SUBLANES == 0
        body = functools.partial(shards, n_tm if line else 1)
        return jax.shard_map(body, mesh=mesh, in_specs=in_specs, out_specs=out_specs, check_vma=False)(*args)

    return step
```

time: 128 us -> 93.1 us (0.73)
  waiting for transfers between devices: 88.6 us -> 49.5 us
  starting transfers between devices: 0.05 us -> 25.4 us
  matrix products: 22.7 us -> 0 us
  Pallas kernels: 0 us -> 16.7 us
  between operations: 14.9 us -> 0.42 us
    all_gather x1 -> x0, waiting for transfers between devices: 61.4 us -> none  [shards(): lax.all_gather(root_coulomb, ('pair', 'tm'), axis=0, tiled=True)]
    ppermute x0 -> x31, waiting for transfers between devices: none -> 49.5 us  [the longest x23 26.3 us: swap(): return lax.ppermute(value, 'pair', [(p, p ^ mask) for p in range(n_pair)])]
    reduce_scatter x1 -> x0, waiting for transfers between devices: 26.5 us -> none  [shards(): chi_flat = lax.psum_scatter(blocks, 'pair', scatter_dimension=0, tiled=True)]
    ppermute x0 -> x31, starting transfers between devices: none -> 25.4 us  [the longest x23 14.3 us: swap(): return lax.ppermute(value, 'pair', [(p, p ^ mask) for p in range(n_pair)])]
    dot_general x5 -> x0, matrix products: 22.7 us -> none  [the longest x1 15.9 us: shards(): lax.dot_general(weighted, three_centre, (((1,), (1,)), ((), ())), preferr...]
    pallas_call x0 -> x7, Pallas kernels: none -> 16.7 us  [the longest x3 7.93 us: partial_rows(): pl.pallas_call(functools.partial(partial_kernel, masks, arrived is not No...]
    reshape x2 -> x0, local copies, waits for them, and re-layouts: 1.52 us -> none  [the longest x1 0.76 us: shards(): occ_table = occ_depth.reshape(NOB, OB)]
  transfers between devices with their start and end apart: 2 -> 31, of which waited for: 2 -> 9; matrix products, arithmetic and copies ran while one was open for 15% -> 0% of each run, Pallas kernels for 0% -> 16%
where the time goes in v1:
time: 93.1 us; the launch traced here: 92.8 us
  waiting for transfers between devices  49.5 us (53%)
  starting transfers between devices  25.4 us (27%)
  Pallas kernels  16.7 us (18%)
    ppermute x23, waiting for transfers between devices, swap(): return lax.ppermute(value, 'pair', [(p, p ^ mask) for p in range(n_pair)])  26.3 us
    ppermute x8, waiting for transfers between devices, along(): return lax.ppermute(value, 'tm', moves)  23.2 us
    ppermute x23, starting transfers between devices, swap(): return lax.ppermute(value, 'pair', [(p, p ^ mask) for p in range(n_pair)])  14.3 us
    ppermute x8, starting transfers between devices, along(): return lax.ppermute(value, 'tm', moves)  11 us
    pallas_call x3, Pallas kernels, partial_rows(): pl.pallas_call(functools.partial(partial_kernel, masks, arrived is not No...  7.93 us
    pallas_call x1, Pallas kernels, first_rows(): pl.pallas_call(functools.partial(first_kernel, taus, coef, layers, masks)...  6.08 us
  transfers between devices with their start and end apart: 31, of which 9 were waited for; matrix products, arithmetic and copies ran while one was open for 0% of the time, Pallas kernels for 16%

profile of v1, /device:TPU:0, one launch (start us, length us, event | category | flops | bytes accessed | tf_op | source)
XLA Modules:
  0.0 92.8 jit_solution(9486087567713727532)
XLA Ops:
  0.0 0.8 slice.19
  0.8 5.1 %collective-permute-start.20 = (bf16[48,512]{1,0:T(8,128)(2,1)S(1)}, bf16[48,512]{1,0:T(8,128)(2,1)S(1)}, u32[]{:S(2)}, u32[]{:S(2)}) collective-permute-start(bf16[48,512]{1,0:T(8,128)(2,1)S(1)} %slice.19), channel_id=1, source_target_pairs={{0,3},{1,2},{2,1},{3,0},{4,7},{5,6},{6,5},{7,4},{8,11},{9,10},{10,... | collective-permute-start | bytes 147464 | tf_op jit(solution)/shard_map/ppermute | solution.py:325
  5.9 0.6 collective-permute-start.18
  6.4 1.6 %collective-permute-done.20 = bf16[48,512]{1,0:T(8,128)(2,1)S(1)} collective-permute-done((bf16[48,512]{1,0:T(8,128)(2,1)S(1)}, bf16[48,512]{1,0:T(8,128)(2,1)S(1)}, u32[]{:S(2)}, u32[]{:S(2)}) %collective-permute-start.20) | collective-permute-done | bytes 49184 | tf_op jit(solution)/shard_map/ppermute | solution.py:325
  8.0 2.9 %collective-permute-done.19 = bf16[48,512]{1,0:T(8,128)(2,1)S(1)} collective-permute-done((bf16[48,512]{1,0:T(8,128)(2,1)S(1)}, bf16[48,512]{1,0:T(8,128)(2,1)S(1)}, u32[]{:S(2)}, u32[]{:S(2)}) %collective-permute-start.19) | collective-permute-done | bytes 49184 | tf_op jit(solution)/shard_map/ppermute | solution.py:325
  10.9 1.6 %collective-permute-start.22 = (bf16[192,512]{1,0:T(8,128)(2,1)S(1)}, bf16[192,512]{1,0:T(8,128)(2,1)S(1)}, u32[]{:S(2)}, u32[]{:S(2)}) collective-permute-start(bf16[192,512]{1,0:T(8,128)(2,1)S(1)} %pad_maximum_fusion.1.refs_8_.refs_4_), channel_id=1, source_target_pairs={{0,8},{4,12},{8,0},{12,4},{16,24},{20,28},{24,16},{28,20},{1,9},{5... | collective-permute-start | bytes 589832 | tf_op jit(solution)/shard_map/ppermute | solution.py:321
  12.4 1.5 %collective-permute-start.9 = (bf16[48,1536]{1,0:T(8,128)(2,1)}, bf16[48,1536]{1,0:T(8,128)(2,1)S(1)}, u32[]{:S(2)}, u32[]{:S(2)}) collective-permute-start(bf16[48,1536]{1,0:T(8,128)(2,1)} %param.7), channel_id=1, source_target_pairs={{0,24},{4,28},{8,16},{12,20},{16,8},{20,12},{24,0},{28,4},{1,25},{... | collective-permute-start | bytes 442376 | tf_op jit(solution)/shard_map/ppermute | solution.py:321
  13.9 0.5 collective-permute-start.8
  14.4 1.5 %collective-permute-start.7 = (bf16[48,1536]{1,0:T(8,128)(2,1)}, bf16[48,1536]{1,0:T(8,128)(2,1)S(1)}, u32[]{:S(2)}, u32[]{:S(2)}) collective-permute-start(bf16[48,1536]{1,0:T(8,128)(2,1)} %param.7), channel_id=1, source_target_pairs={{0,8},{4,12},{8,0},{12,4},{16,24},{20,28},{24,16},{28,20},{1,9},{5... | collective-permute-start | bytes 442376 | tf_op jit(solution)/shard_map/ppermute | solution.py:321
  15.9 6.6 %collective-permute-done.9 = bf16[48,1536]{1,0:T(8,128)(2,1)S(1)} collective-permute-done((bf16[48,1536]{1,0:T(8,128)(2,1)}, bf16[48,1536]{1,0:T(8,128)(2,1)S(1)}, u32[]{:S(2)}, u32[]{:S(2)}) %collective-permute-start.9) | collective-permute-done | bytes 147488 | tf_op jit(solution)/shard_map/ppermute | solution.py:321
  22.5 0.5 collective-permute-start.24
  23.0 2.5 %collective-permute-start.26 = (bf16[192,512]{1,0:T(8,128)(2,1)S(1)}, bf16[192,512]{1,0:T(8,128)(2,1)S(1)}, u32[]{:S(2)}, u32[]{:S(2)}) collective-permute-start(bf16[192,512]{1,0:T(8,128)(2,1)S(1)} %pad_maximum_fusion.1.refs_8_.refs_4_), channel_id=1, source_target_pairs={{0,24},{4,28},{8,16},{12,20},{16,8},{20,12},{24,0},{28,4},{1,25},{... | collective-permute-start | bytes 589832 | tf_op jit(solution)/shard_map/ppermute | solution.py:321
  25.5 6.1 %first.1 = (f32[8,256]{1,0:T(8,128)S(1)}, bf16[1536,2048]{1,0:T(8,128)(2,1)S(1)}, bf16[192,1536]{1,0:T(8,128)(2,1)S(1)}, bf16[192,1536]{1,0:T(8,128)(2,1)S(1)}) custom-call(s32[8]{0:T(128)} %occ_block.1, s32[8]{0:T(128)} %vir_block.1, f32[1,256]{1,0:T(1,128)} %bitcast.3, f32[1,1024]{1,0:T(1,128)} %bitcast.2, bf16[1536,2048]{1,0:T(8,128)(2,1)} %source.1), custom_call_target="tpu_custom_call" | custom-call | flops 2415919104 | bytes 6291456 | tf_op jit(solution)/shard_map/first/pallas_call | solution.py:144
  32.2 1.3 %collective-permute-start.11 = (bf16[192,1024]{1,0:T(8,128)(2,1)S(1)}, bf16[192,1024]{1,0:T(8,128)(2,1)S(1)}, u32[]{:S(2)}, u32[]{:S(2)}) collective-permute-start(bf16[192,1024]{1,0:T(8,128)(2,1)S(1)} %pad_maximum_fusion.refs_0_), channel_id=1, source_target_pairs={{0,1},{1,0},{2,3},{3,2},{4,5},{5,4},{6,7},{7,6},{8,9},{9,8},{10,11... | collective-permute-start | bytes 1179656 | tf_op jit(solution)/shard_map/ppermute | solution.py:325
  33.5 0.7 collective-permute-start.15
  34.7 2.6 %partial.4 = (bf16[192,1536]{1,0:T(8,128)(2,1)S(1)}, bf16[192,1536]{1,0:T(8,128)(2,1)S(1)}) custom-call(f32[8,256]{1,0:T(8,128)S(1)} %get-tuple-element.17.w_ref, bf16[1536,2048]{1,0:T(8,128)(2,1)S(1)} %get-tuple-element.18.held), custom_call_target="tpu_custom_call" | custom-call | flops 2415919104 | bytes 10223616 | tf_op jit(solution)/shard_map/partial/pallas_call | solution.py:190
  38.0 5.4 %collective-permute-done.11.refs_2_ = bf16[192,1024]{1,0:T(8,128)(2,1)S(1)} collective-permute-done((bf16[192,1024]{1,0:T(8,128)(2,1)S(1)}, bf16[192,1024]{1,0:T(8,128)(2,1)S(1)}, u32[]{:S(2)}, u32[]{:S(2)}) %collective-permute-start.11) | collective-permute-done | bytes 393248 | tf_op jit(solution)/shard_map/ppermute | solution.py:325
  43.4 0.7 collective-permute-start.13
  44.2 1.3 %collective-permute-start.16 = (bf16[192,1024]{1,0:T(8,128)(2,1)S(1)}, bf16[192,1024]{1,0:T(8,128)(2,1)S(1)}, u32[]{:S(2)}, u32[]{:S(2)}) collective-permute-start(bf16[192,1024]{1,0:T(8,128)(2,1)S(1)} %collective-permute-done.15.refs_0_), channel_id=1, source_target_pairs={{1,0},{2,3},{5,4},{6,7},{9,8},{10,11},{13,12},{14,15},{17,16},{18,... | collective-permute-start | bytes 1179656 | tf_op jit(solution)/shard_map/ppermute | solution.py:325
  45.5 0.5 collective-permute-start.10
  46.6 2.6 %partial.3 = (bf16[192,1536]{1,0:T(8,128)(2,1)S(1)}, bf16[192,1536]{1,0:T(8,128)(2,1)S(1)}) custom-call(f32[8,256]{1,0:T(8,128)S(1)} %get-tuple-element.17.w_ref, bf16[1536,2048]{1,0:T(8,128)(2,1)S(1)} %get-tuple-element.18.held, bf16[192,1536]{1,0:T(8,128)(2,1)S(1)} %collective-permute-done.refs_0_, bf16[192,1536]{1,0:T(8,128)(2,1)S(1)} %collective-permute-done.1.refs_1_), custom_call_target="tpu_custom_call" | custom-call | flops 2415919104 | bytes 10223616 | tf_op jit(solution)/shard_map/partial/pallas_call | solution.py:190
  49.2 1.5 %collective-permute-start.29 = (bf16[192,1024]{1,0:T(8,128)(2,1)S(1)}, bf16[192,1024]{1,0:T(8,128)(2,1)S(1)}, u32[]{:S(2)}, u32[]{:S(2)}) collective-permute-start(bf16[192,1024]{1,0:T(8,128)(2,1)S(1)} %collective-permute-done.13.refs_4_), channel_id=1, source_target_pairs={{1,0},{2,3},{5,4},{6,7},{9,8},{10,11},{13,12},{14,15},{17,16},{18,... | collective-permute-start | bytes 1179656 | tf_op jit(solution)/shard_map/ppermute | solution.py:325
  50.7 7.5 %collective-permute-done.16.refs_6_ = bf16[192,1024]{1,0:T(8,128)(2,1)S(1)} collective-permute-done((bf16[192,1024]{1,0:T(8,128)(2,1)S(1)}, bf16[192,1024]{1,0:T(8,128)(2,1)S(1)}, u32[]{:S(2)}, u32[]{:S(2)}) %collective-permute-start.16) | collective-permute-done | bytes 393248 | tf_op jit(solution)/shard_map/ppermute | solution.py:325
  58.2 2.6 %partial.5 = (bf16[192,1536]{1,0:T(8,128)(2,1)S(1)}, f32[192,1536]{1,0:T(8,128)S(1)}) custom-call(f32[8,256]{1,0:T(8,128)S(1)} %get-tuple-element.17.w_ref, bf16[1536,2048]{1,0:T(8,128)(2,1)S(1)} %get-tuple-element.18.held, bf16[192,1536]{1,0:T(8,128)(2,1)S(1)} %collective-permute-done.4.refs_0_, bf16[192,1536]{1,0:T(8,128)(2,1)S(1)} %collective-permute-done.5.refs_1_), custom_call_target="tpu_custom_call" | custom-call | flops 2415919104 | bytes 10223616 | tf_op jit(solution)/shard_map/partial/pallas_call | solution.py:190
  61.3 1.4 %collective-permute-start.3 = (bf16[192,1536]{1,0:T(8,128)(2,1)S(1)}, bf16[192,1536]{1,0:T(8,128)(2,1)S(1)}, u32[]{:S(2)}, u32[]{:S(2)}) collective-permute-start(bf16[192,1536]{1,0:T(8,128)(2,1)S(1)} %get-tuple-element.22), channel_id=1, source_target_pairs={{0,8},{4,12},{8,0},{12,4},{16,24},{20,28},{24,16},{28,20},{1,9},{5... | collective-permute-start | bytes 1769480 | tf_op jit(solution)/shard_map/ppermute | solution.py:321
  62.7 1.8 %collective-permute-start.6 = (bf16[192,1536]{1,0:T(8,128)(2,1)S(1)}, bf16[192,1536]{1,0:T(8,128)(2,1)S(1)}, u32[]{:S(2)}, u32[]{:S(2)}) collective-permute-start(bf16[192,1536]{1,0:T(8,128)(2,1)S(1)} %get-tuple-element.25), channel_id=1, source_target_pairs={{0,16},{4,20},{8,24},{12,28},{16,0},{20,4},{24,8},{28,12},{1,17},{... | collective-permute-start | bytes 1769480 | tf_op jit(solution)/shard_map/ppermute | solution.py:321
  64.5 5.8 %collective-permute-done.29.refs_2_ = bf16[192,1024]{1,0:T(8,128)(2,1)S(1)} collective-permute-done((bf16[192,1024]{1,0:T(8,128)(2,1)S(1)}, bf16[192,1024]{1,0:T(8,128)(2,1)S(1)}, u32[]{:S(2)}, u32[]{:S(2)}) %collective-permute-start.29) | collective-permute-done | bytes 393248 | tf_op jit(solution)/shard_map/ppermute | solution.py:325
  70.6 7.5 %collective-permute-done.2.refs_0_ = bf16[192,1536]{1,0:T(8,128)(2,1)S(1)} collective-permute-done((bf16[192,1536]{1,0:T(8,128)(2,1)S(1)}, bf16[192,1536]{1,0:T(8,128)(2,1)S(1)}, u32[]{:S(2)}, u32[]{:S(2)}) %collective-permute-start.2) | collective-permute-done | bytes 589856 | tf_op jit(solution)/shard_map/ppermute | solution.py:321
  78.1 11.0 %collective-permute-done.3.refs_1_ = bf16[192,1536]{1,0:T(8,128)(2,1)S(1)} collective-permute-done((bf16[192,1536]{1,0:T(8,128)(2,1)S(1)}, bf16[192,1536]{1,0:T(8,128)(2,1)S(1)}, u32[]{:S(2)}, u32[]{:S(2)}) %collective-permute-start.3) | collective-permute-done | bytes 589856 | tf_op jit(solution)/shard_map/ppermute | solution.py:321
  89.1 1.2 %collective-permute-done.6.refs_2_ = bf16[192,1536]{1,0:T(8,128)(2,1)S(1)} collective-permute-done((bf16[192,1536]{1,0:T(8,128)(2,1)S(1)}, bf16[192,1536]{1,0:T(8,128)(2,1)S(1)}, u32[]{:S(2)}, u32[]{:S(2)}) %collective-permute-start.6) | collective-permute-done | bytes 589856 | tf_op jit(solution)/shard_map/ppermute | solution.py:321
  90.2 1.0 %screen.1 = (f32[192,1536]{1,0:T(8,128)S(1)}, bf16[192,1536]{1,0:T(8,128)(2,1)S(1)}) custom-call(bf16[192,1536]{1,0:T(8,128)(2,1)S(1)} %collective-permute-done.2.refs_0_, bf16[192,1536]{1,0:T(8,128)(2,1)S(1)} %collective-permute-done.3.refs_1_, bf16[192,1536]{1,0:T(8,128)(2,1)S(1)} %collective-permute-done.6.refs_2_, ...), custom_call_target="tpu_custom_call" | custom-call | flops 679477248 | bytes 5308416 | tf_op jit(solution)/shard_map/screen/pallas_call | solution.py:263
  91.3 1.4 %finish.1 = f32[1,192,1536]{2,1,0:T(8,128)} custom-call(f32[192,1536]{1,0:T(8,128)S(1)} %get-tuple-element.27.total, bf16[192,1536]{1,0:T(8,128)(2,1)S(1)} %get-tuple-element.28.chi, bf16[192,1024]{1,0:T(8,128)(2,1)S(1)} %collective-permute-done.15.refs_0_, bf16[192,1024]{1,0:T(8,128)(2,1)S(1)} %collective-permute-done.28.refs_1_, ...), custom_call_target="tpu_custom_call" | custom-call | flops 226492416 | bytes 3538944 | tf_op jit(solution)/shard_map/finish/pallas_call | solution.py:301
  (46 shorter events, 3.0 us)
Async XLA Ops:
  0.8 7.2 %collective-permute-start.20 = (bf16[48,512]{1,0:T(8,128)(2,1)S(1)}, bf16[48,512]{1,0:T(8,128)(2,1)S(1)}, u32[]{:S(2)}, u32[]{:S(2)}) collective-permute-start(bf16[48,512]{1,0:T(8,128)(2,1)S(1)} %slice.19), channel_id=1, source_target_pairs={{0,3},{1,2},{2,1},{3,0},{4,7},{5,6},{6,5},{7,4},{8,11},{9,10},{10,... | collective-permute-start | bytes 147464 | tf_op jit(solution)/shard_map/ppermute | solution.py:325
  5.9 5.0 %collective-permute-start.19 = (bf16[48,512]{1,0:T(8,128)(2,1)S(1)}, bf16[48,512]{1,0:T(8,128)(2,1)S(1)}, u32[]{:S(2)}, u32[]{:S(2)}) collective-permute-start(bf16[48,512]{1,0:T(8,128)(2,1)S(1)} %slice.19), channel_id=1, source_target_pairs={{0,2},{1,3},{2,0},{3,1},{4,6},{5,7},{6,4},{7,5},{8,10},{9,11},{10,... | collective-permute-start | bytes 147464 | tf_op jit(solution)/shard_map/ppermute | solution.py:325
  5.9 5.0 %collective-permute-start.18 = (bf16[48,512]{1,0:T(8,128)(2,1)S(1)}, bf16[48,512]{1,0:T(8,128)(2,1)S(1)}, u32[]{:S(2)}, u32[]{:S(2)}) collective-permute-start(bf16[48,512]{1,0:T(8,128)(2,1)S(1)} %slice.19), channel_id=1, source_target_pairs={{0,1},{1,0},{2,3},{3,2},{4,5},{5,4},{6,7},{7,6},{8,9},{9,8},{10,11... | collective-permute-start | bytes 147464 | tf_op jit(solution)/shard_map/ppermute | solution.py:325
  10.9 14.6 %collective-permute-start.22 = (bf16[192,512]{1,0:T(8,128)(2,1)S(1)}, bf16[192,512]{1,0:T(8,128)(2,1)S(1)}, u32[]{:S(2)}, u32[]{:S(2)}) collective-permute-start(bf16[192,512]{1,0:T(8,128)(2,1)S(1)} %pad_maximum_fusion.1.refs_8_.refs_4_), channel_id=1, source_target_pairs={{0,8},{4,12},{8,0},{12,4},{16,24},{20,28},{24,16},{28,20},{1,9},{5... | collective-permute-start | bytes 589832 | tf_op jit(solution)/shard_map/ppermute | solution.py:321
  12.4 10.1 %collective-permute-start.9 = (bf16[48,1536]{1,0:T(8,128)(2,1)}, bf16[48,1536]{1,0:T(8,128)(2,1)S(1)}, u32[]{:S(2)}, u32[]{:S(2)}) collective-permute-start(bf16[48,1536]{1,0:T(8,128)(2,1)} %param.7), channel_id=1, source_target_pairs={{0,24},{4,28},{8,16},{12,20},{16,8},{20,12},{24,0},{28,4},{1,25},{... | collective-permute-start | bytes 442376 | tf_op jit(solution)/shard_map/ppermute | solution.py:321
  13.9 9.1 %collective-permute-start.8 = (bf16[48,1536]{1,0:T(8,128)(2,1)}, bf16[48,1536]{1,0:T(8,128)(2,1)S(1)}, u32[]{:S(2)}, u32[]{:S(2)}) collective-permute-start(bf16[48,1536]{1,0:T(8,128)(2,1)} %param.7), channel_id=1, source_target_pairs={{0,16},{4,20},{8,24},{12,28},{16,0},{20,4},{24,8},{28,12},{1,17},{... | collective-permute-start | bytes 442376 | tf_op jit(solution)/shard_map/ppermute | solution.py:321
  14.4 17.2 %collective-permute-start.7 = (bf16[48,1536]{1,0:T(8,128)(2,1)}, bf16[48,1536]{1,0:T(8,128)(2,1)S(1)}, u32[]{:S(2)}, u32[]{:S(2)}) collective-permute-start(bf16[48,1536]{1,0:T(8,128)(2,1)} %param.7), channel_id=1, source_target_pairs={{0,8},{4,12},{8,0},{12,4},{16,24},{20,28},{24,16},{28,20},{1,9},{5... | collective-permute-start | bytes 442376 | tf_op jit(solution)/shard_map/ppermute | solution.py:321
  15.9 16.3 %collective-permute-start.21 = (bf16[192,512]{1,0:T(8,128)(2,1)S(1)}, bf16[192,512]{1,0:T(8,128)(2,1)S(1)}, u32[]{:S(2)}, u32[]{:S(2)}) collective-permute-start(bf16[192,512]{1,0:T(8,128)(2,1)S(1)} %pad_maximum_fusion.1.refs_8_.refs_4_), channel_id=1, source_target_pairs={{0,4},{4,0},{8,12},{12,8},{16,20},{20,16},{24,28},{28,24},{1,5},{5... | collective-permute-start | bytes 589832 | tf_op jit(solution)/shard_map/ppermute | solution.py:321
  22.5 11.0 %collective-permute-start.24 = (bf16[192,512]{1,0:T(8,128)(2,1)S(1)}, bf16[192,512]{1,0:T(8,128)(2,1)S(1)}, u32[]{:S(2)}, u32[]{:S(2)}) collective-permute-start(bf16[192,512]{1,0:T(8,128)(2,1)S(1)} %pad_maximum_fusion.1.refs_8_.refs_4_), channel_id=1, source_target_pairs={{0,16},{4,20},{8,24},{12,28},{16,0},{20,4},{24,8},{28,12},{1,17},{... | collective-permute-start | bytes 589832 | tf_op jit(solution)/shard_map/ppermute | solution.py:321
  23.0 11.1 %collective-permute-start.26 = (bf16[192,512]{1,0:T(8,128)(2,1)S(1)}, bf16[192,512]{1,0:T(8,128)(2,1)S(1)}, u32[]{:S(2)}, u32[]{:S(2)}) collective-permute-start(bf16[192,512]{1,0:T(8,128)(2,1)S(1)} %pad_maximum_fusion.1.refs_8_.refs_4_), channel_id=1, source_target_pairs={{0,24},{4,28},{8,16},{12,20},{16,8},{20,12},{24,0},{28,4},{1,25},{... | collective-permute-start | bytes 589832 | tf_op jit(solution)/shard_map/ppermute | solution.py:321
  25.5 8.7 %collective-permute-start.23 = (bf16[192,512]{1,0:T(8,128)(2,1)S(1)}, bf16[192,512]{1,0:T(8,128)(2,1)S(1)}, u32[]{:S(2)}, u32[]{:S(2)}) collective-permute-start(bf16[192,512]{1,0:T(8,128)(2,1)S(1)} %collective-permute-done.22.refs_10_.refs_6_), channel_id=1, source_target_pairs={{0,4},{4,0},{8,12},{12,8},{16,20},{20,16},{24,28},{28,24},{1,5},{5... | collective-permute-start | bytes 589832 | tf_op jit(solution)/shard_map/ppermute | solution.py:321
  25.5 6.1 %copy-start = (bf16[48,1536]{1,0:T(8,128)(2,1)S(1)}, bf16[48,1536]{1,0:T(8,128)(2,1)}, u32[]{:S(2)}) copy-start(bf16[48,1536]{1,0:T(8,128)(2,1)} %param.7) | copy-start | bytes 442372
  31.7 12.5 %collective-permute-start = (bf16[192,1536]{1,0:T(8,128)(2,1)S(1)}, bf16[192,1536]{1,0:T(8,128)(2,1)S(1)}, u32[]{:S(2)}, u32[]{:S(2)}) collective-permute-start(bf16[192,1536]{1,0:T(8,128)(2,1)S(1)} %get-tuple-element.19), channel_id=1, source_target_pairs={{0,4},{4,0},{8,12},{12,8},{16,20},{20,16},{24,28},{28,24},{1,5},{5... | collective-permute-start | bytes 1769480 | tf_op jit(solution)/shard_map/ppermute | solution.py:321
  32.2 11.2 %collective-permute-start.11 = (bf16[192,1024]{1,0:T(8,128)(2,1)S(1)}, bf16[192,1024]{1,0:T(8,128)(2,1)S(1)}, u32[]{:S(2)}, u32[]{:S(2)}) collective-permute-start(bf16[192,1024]{1,0:T(8,128)(2,1)S(1)} %pad_maximum_fusion.refs_0_), channel_id=1, source_target_pairs={{0,1},{1,0},{2,3},{3,2},{4,5},{5,4},{6,7},{7,6},{8,9},{9,8},{10,11... | collective-permute-start | bytes 1179656 | tf_op jit(solution)/shard_map/ppermute | solution.py:325
  33.5 10.6 %collective-permute-start.15 = (bf16[192,1024]{1,0:T(8,128)(2,1)S(1)}, bf16[192,1024]{1,0:T(8,128)(2,1)S(1)}, u32[]{:S(2)}, u32[]{:S(2)}) collective-permute-start(bf16[192,1024]{1,0:T(8,128)(2,1)S(1)} %pad_maximum_fusion.refs_0_), channel_id=1, source_target_pairs={{1,2},{2,1},{5,6},{6,5},{9,10},{10,9},{13,14},{14,13},{17,18},{18,... | collective-permute-start | bytes 1179656 | tf_op jit(solution)/shard_map/ppermute | solution.py:325
  34.1 3.2 %collective-permute-start.25 = (bf16[192,512]{1,0:T(8,128)(2,1)S(1)}, bf16[192,512]{1,0:T(8,128)(2,1)S(1)}, u32[]{:S(2)}, u32[]{:S(2)}) collective-permute-start(bf16[192,512]{1,0:T(8,128)(2,1)S(1)} %collective-permute-done.24.refs_12_.refs_8_), channel_id=1, source_target_pairs={{0,4},{4,0},{8,12},{12,8},{16,20},{20,16},{24,28},{28,24},{1,5},{5... | collective-permute-start | bytes 589832 | tf_op jit(solution)/shard_map/ppermute | solution.py:321
  34.2 3.3 %collective-permute-start.27 = (bf16[192,512]{1,0:T(8,128)(2,1)S(1)}, bf16[192,512]{1,0:T(8,128)(2,1)S(1)}, u32[]{:S(2)}, u32[]{:S(2)}) collective-permute-start(bf16[192,512]{1,0:T(8,128)(2,1)S(1)} %collective-permute-done.26.refs_14_.refs_10_), channel_id=1, source_target_pairs={{0,4},{4,0},{8,12},{12,8},{16,20},{20,16},{24,28},{28,24},{1,5},{5... | collective-permute-start | bytes 589832 | tf_op jit(solution)/shard_map/ppermute | solution.py:321
  37.4 8.1 %collective-permute-start.1 = (bf16[192,1536]{1,0:T(8,128)(2,1)S(1)}, bf16[192,1536]{1,0:T(8,128)(2,1)S(1)}, u32[]{:S(2)}, u32[]{:S(2)}) collective-permute-start(bf16[192,1536]{1,0:T(8,128)(2,1)S(1)} %get-tuple-element.20), channel_id=1, source_target_pairs={{0,4},{4,0},{8,12},{12,8},{16,20},{20,16},{24,28},{28,24},{1,5},{5... | collective-permute-start | bytes 1769480 | tf_op jit(solution)/shard_map/ppermute | solution.py:321
  37.5 8.5 %collective-permute-start.4 = (bf16[192,1536]{1,0:T(8,128)(2,1)S(1)}, bf16[192,1536]{1,0:T(8,128)(2,1)S(1)}, u32[]{:S(2)}, u32[]{:S(2)}) collective-permute-start(bf16[192,1536]{1,0:T(8,128)(2,1)S(1)} %get-tuple-element.23), channel_id=1, source_target_pairs={{0,4},{4,0},{8,12},{12,8},{16,20},{20,16},{24,28},{28,24},{1,5},{5... | collective-permute-start | bytes 1769480 | tf_op jit(solution)/shard_map/ppermute | solution.py:321
  43.4 2.7 %collective-permute-start.13 = (bf16[192,1024]{1,0:T(8,128)(2,1)S(1)}, bf16[192,1024]{1,0:T(8,128)(2,1)S(1)}, u32[]{:S(2)}, u32[]{:S(2)}) collective-permute-start(bf16[192,1024]{1,0:T(8,128)(2,1)S(1)} %collective-permute-done.11.refs_2_), channel_id=1, source_target_pairs={{1,2},{2,1},{5,6},{6,5},{9,10},{10,9},{13,14},{14,13},{17,18},{18,... | collective-permute-start | bytes 1179656 | tf_op jit(solution)/shard_map/ppermute | solution.py:325
  44.1 5.1 %collective-permute-start.5 = (bf16[192,1536]{1,0:T(8,128)(2,1)S(1)}, bf16[192,1536]{1,0:T(8,128)(2,1)S(1)}, u32[]{:S(2)}, u32[]{:S(2)}) collective-permute-start(bf16[192,1536]{1,0:T(8,128)(2,1)S(1)} %get-tuple-element.24), channel_id=1, source_target_pairs={{0,4},{4,0},{8,12},{12,8},{16,20},{20,16},{24,28},{28,24},{1,5},{5... | collective-permute-start | bytes 1769480 | tf_op jit(solution)/shard_map/ppermute | solution.py:321
  44.2 14.1 %collective-permute-start.16 = (bf16[192,1024]{1,0:T(8,128)(2,1)S(1)}, bf16[192,1024]{1,0:T(8,128)(2,1)S(1)}, u32[]{:S(2)}, u32[]{:S(2)}) collective-permute-start(bf16[192,1024]{1,0:T(8,128)(2,1)S(1)} %collective-permute-done.15.refs_0_), channel_id=1, source_target_pairs={{1,0},{2,3},{5,4},{6,7},{9,8},{10,11},{13,12},{14,15},{17,16},{18,... | collective-permute-start | bytes 1179656 | tf_op jit(solution)/shard_map/ppermute | solution.py:325
  45.5 15.4 %collective-permute-start.10 = (bf16[192,1024]{1,0:T(8,128)(2,1)S(1)}, bf16[192,1024]{1,0:T(8,128)(2,1)S(1)}, u32[]{:S(2)}, u32[]{:S(2)}) collective-permute-start(bf16[192,1024]{1,0:T(8,128)(2,1)S(1)} %pad_maximum_fusion.refs_0_), channel_id=1, source_target_pairs={{0,4},{4,0},{8,12},{12,8},{16,20},{20,16},{24,28},{28,24},{1,5},{5... | collective-permute-start | bytes 1179656 | tf_op jit(solution)/shard_map/ppermute | solution.py:321
  46.0 15.3 %collective-permute-start.12 = (bf16[192,1024]{1,0:T(8,128)(2,1)S(1)}, bf16[192,1024]{1,0:T(8,128)(2,1)S(1)}, u32[]{:S(2)}, u32[]{:S(2)}) collective-permute-start(bf16[192,1024]{1,0:T(8,128)(2,1)S(1)} %collective-permute-done.11.refs_2_), channel_id=1, source_target_pairs={{0,4},{4,0},{8,12},{12,8},{16,20},{20,16},{24,28},{28,24},{1,5},{5... | collective-permute-start | bytes 1179656 | tf_op jit(solution)/shard_map/ppermute | solution.py:321
  46.1 16.6 %collective-permute-start.14 = (bf16[192,1024]{1,0:T(8,128)(2,1)S(1)}, bf16[192,1024]{1,0:T(8,128)(2,1)S(1)}, u32[]{:S(2)}, u32[]{:S(2)}) collective-permute-start(bf16[192,1024]{1,0:T(8,128)(2,1)S(1)} %collective-permute-done.13.refs_4_), channel_id=1, source_target_pairs={{0,4},{4,0},{8,12},{12,8},{16,20},{20,16},{24,28},{28,24},{1,5},{5... | collective-permute-start | bytes 1179656 | tf_op jit(solution)/shard_map/ppermute | solution.py:321
  49.2 21.1 %collective-permute-start.29 = (bf16[192,1024]{1,0:T(8,128)(2,1)S(1)}, bf16[192,1024]{1,0:T(8,128)(2,1)S(1)}, u32[]{:S(2)}, u32[]{:S(2)}) collective-permute-start(bf16[192,1024]{1,0:T(8,128)(2,1)S(1)} %collective-permute-done.13.refs_4_), channel_id=1, source_target_pairs={{1,0},{2,3},{5,4},{6,7},{9,8},{10,11},{13,12},{14,15},{17,16},{18,... | collective-permute-start | bytes 1179656 | tf_op jit(solution)/shard_map/ppermute | solution.py:325
  58.2 6.2 %collective-permute-start.17 = (bf16[192,1024]{1,0:T(8,128)(2,1)S(1)}, bf16[192,1024]{1,0:T(8,128)(2,1)S(1)}, u32[]{:S(2)}, u32[]{:S(2)}) collective-permute-start(bf16[192,1024]{1,0:T(8,128)(2,1)S(1)} %collective-permute-done.16.refs_6_), channel_id=1, source_target_pairs={{0,4},{4,0},{8,12},{12,8},{16,20},{20,16},{24,28},{28,24},{1,5},{5... | collective-permute-start | bytes 1179656 | tf_op jit(solution)/shard_map/ppermute | solution.py:321
  60.9 17.2 %collective-permute-start.2 = (bf16[192,1536]{1,0:T(8,128)(2,1)S(1)}, bf16[192,1536]{1,0:T(8,128)(2,1)S(1)}, u32[]{:S(2)}, u32[]{:S(2)}) collective-permute-start(bf16[192,1536]{1,0:T(8,128)(2,1)S(1)} %get-tuple-element.21), channel_id=1, source_target_pairs={{0,24},{4,28},{8,16},{12,20},{16,8},{20,12},{24,0},{28,4},{1,25},{... | collective-permute-start | bytes 1769480 | tf_op jit(solution)/shard_map/ppermute | solution.py:321
  61.3 27.8 %collective-permute-start.3 = (bf16[192,1536]{1,0:T(8,128)(2,1)S(1)}, bf16[192,1536]{1,0:T(8,128)(2,1)S(1)}, u32[]{:S(2)}, u32[]{:S(2)}) collective-permute-start(bf16[192,1536]{1,0:T(8,128)(2,1)S(1)} %get-tuple-element.22), channel_id=1, source_target_pairs={{0,8},{4,12},{8,0},{12,4},{16,24},{20,28},{24,16},{28,20},{1,9},{5... | collective-permute-start | bytes 1769480 | tf_op jit(solution)/shard_map/ppermute | solution.py:321
  62.7 27.6 %collective-permute-start.6 = (bf16[192,1536]{1,0:T(8,128)(2,1)S(1)}, bf16[192,1536]{1,0:T(8,128)(2,1)S(1)}, u32[]{:S(2)}, u32[]{:S(2)}) collective-permute-start(bf16[192,1536]{1,0:T(8,128)(2,1)S(1)} %get-tuple-element.25), channel_id=1, source_target_pairs={{0,16},{4,20},{8,24},{12,28},{16,0},{20,4},{24,8},{28,12},{1,17},{... | collective-permute-start | bytes 1769480 | tf_op jit(solution)/shard_map/ppermute | solution.py:321
  64.5 26.8 %collective-permute-start.28 = (bf16[192,1024]{1,0:T(8,128)(2,1)S(1)}, bf16[192,1024]{1,0:T(8,128)(2,1)S(1)}, u32[]{:S(2)}, u32[]{:S(2)}) collective-permute-start(bf16[192,1024]{1,0:T(8,128)(2,1)S(1)} %collective-permute-done.15.refs_0_), channel_id=1, source_target_pairs={{0,4},{4,0},{8,12},{12,8},{16,20},{20,16},{24,28},{28,24},{1,5},{5... | collective-permute-start | bytes 1179656 | tf_op jit(solution)/shard_map/ppermute | solution.py:321
  70.3 21.0 %collective-permute-start.30 = (bf16[192,1024]{1,0:T(8,128)(2,1)S(1)}, bf16[192,1024]{1,0:T(8,128)(2,1)S(1)}, u32[]{:S(2)}, u32[]{:S(2)}) collective-permute-start(bf16[192,1024]{1,0:T(8,128)(2,1)S(1)} %collective-permute-done.29.refs_2_), channel_id=1, source_target_pairs={{0,4},{4,0},{8,12},{12,8},{16,20},{20,16},{24,28},{28,24},{1,5},{5... | collective-permute-start | bytes 1179656 | tf_op jit(solution)/shard_map/ppermute | solution.py:321

commit v2 on v1

--- a/solution.py
+++ b/solution.py
@@ -16,7 +16,7 @@
 LANES = 128
 SUBLANES = 16
 TILE = 512
-SPLIT = 512
+SPLIT = 768
 
 
 AXES = ("pair", "tm")
@@ -80,14 +80,11 @@
         scaled[new, cols] = (source(cols).astype(jnp.float32) * w_ref[k : k + 1, :]).astype(jnp.bfloat16)
 
 
-def multiply(scaled, right, here, outs, arrived=None):
+def multiply(scaled, right, here, out, arrived=None):
     total = lax.dot_general(scaled[...], right, (((1,), (1,)), ((), ())), preferred_element_type=jnp.float32)
-    rows = outs[0].shape[0]
-    for b, out in enumerate(outs):
-        value = total[b * rows : (b + 1) * rows]
-        if arrived:
-            value += arrived[b][:, here].astype(jnp.float32)
-        out[:, here] = value.astype(out.dtype)
+    if arrived is not None:
+        total += arrived[:, here].astype(jnp.float32)
+    out[:, here] = total.astype(out.dtype)
 
 
 def blocks_of(layers, n_pair, naux, z):
@@ -101,17 +98,17 @@
     ]
 
 
-def first_kernel(taus, coef, layers, masks, occ_block, vir_block, occ, vir, source, *refs):
+def first_kernel(taus, coef, layers, masks, rows, first, occ_block, vir_block, occ, vir, source, *refs):
     count = len(masks)
-    w_ref, held, outs = refs[0], refs[1], refs[2 : 2 + count]
-    occ_b, vir_b, occ_t, vir_t, left, scaled, sems = refs[2 + count :]
-    naux, rows = held.shape[0], outs[0].shape[0]
+    w_ref, held, out = refs[:3]
+    occ_b, vir_b, occ_t, vir_t, left, scaled, sems = refs[3:]
+    naux = held.shape[0]
     me, z, n_pair = lax.axis_index("pair"), lax.axis_index("tm"), lax.axis_size("pair")
     small = ((occ_block, occ_b), (vir_block, vir_b), (occ, occ_t), (vir, vir_t))
     pairs = list(small)
     for b, mask in enumerate(masks):
-        first = pl.multiple_of(jnp.bitwise_xor(me, mask) * rows, SUBLANES)
-        pairs.append((source.at[pl.ds(first, rows), :], left.at[pl.ds(b * rows, rows), :]))
+        start = pl.multiple_of(jnp.bitwise_xor(me, mask) * rows, SUBLANES)
+        pairs.append((source.at[pl.ds(start, rows), :], left.at[pl.ds(b * rows, rows), :]))
     blocks = blocks_of(layers, n_pair, naux, z)
     for old, new, length in blocks:
         pairs.append((source.at[pl.ds(pl.multiple_of(old, SUBLANES), length), :], held.at[pl.ds(new, length), :]))
@@ -126,30 +123,32 @@
         here = pl.ds(b * rows, rows)
         scale_rows(scaled, here, lambda cols: left[here, cols], w_ref)
     waiting = list(zip(copies[len(small) + count :], blocks))
-    tile = math.gcd(naux, TILE)
-    for n in range(naux // tile):
-        while waiting and waiting[0][1][1] < (n + 1) * tile:
+    width = out.shape[1]
+    tile = math.gcd(width, TILE)
+    for n in range(width // tile):
+        while waiting and waiting[0][1][1] < first + (n + 1) * tile:
             waiting.pop(0)[0].wait()
-        here = pl.ds(n * tile, tile)
-        multiply(scaled, held[here, :], here, outs)
-
-
-def first_rows(three_centre, occ_depth, vir_energy, occ_block, vir_block, masks, rows, layers, n_times):
+        multiply(scaled, held[pl.ds(first + n * tile, tile), :], pl.ds(n * tile, tile), out)
+    for copy, _ in waiting:
+        copy.wait()
+
+
+def first_rows(three_centre, occ_depth, vir_energy, occ_block, vir_block, masks, rows, layers, n_times, first, width):
     taus, coef = time_tables(n_times)
-    naux, depth = three_centre.shape
+    _, depth = three_centre.shape
     count = len(masks)
     vmem = pl.BlockSpec(memory_space=pltpu.VMEM)
     operands = (occ_block, vir_block, occ_depth.reshape(1, -1), vir_energy.reshape(1, -1), three_centre)
     n_copies = 4 + count + (1 if layers == 1 else layers * lax.axis_size("pair"))
-    results = pl.pallas_call(
-        functools.partial(first_kernel, taus, coef, layers, masks),
+    return pl.pallas_call(
+        functools.partial(first_kernel, taus, coef, layers, masks, rows, first),
         out_shape=[
             pltpu.VMEM((occ_block.shape[0], OB * VB), jnp.float32),
             pltpu.VMEM(three_centre.shape, three_centre.dtype),
-        ]
-        + [jax.ShapeDtypeStruct((rows, naux), jnp.bfloat16)] * count,
+            jax.ShapeDtypeStruct((count * rows, width), jnp.bfloat16),
+        ],
         in_specs=[pl.BlockSpec(memory_space=pltpu.HBM)] * len(operands),
-        out_specs=[vmem] * (2 + count),
+        out_specs=[vmem] * 3,
         scratch_shapes=[pltpu.SMEM(occ_block.shape, jnp.int32), pltpu.SMEM(vir_block.shape, jnp.int32)]
         + [pltpu.VMEM(v.shape, jnp.float32) for v in operands[2:4]]
         + [pltpu.VMEM((count * rows, depth), jnp.bfloat16)] * 2
@@ -157,17 +156,16 @@
         name="first",
         compiler_params=pltpu.CompilerParams(vmem_limit_bytes=24 * 2**20),
         cost_estimate=pl.CostEstimate(
-            flops=2 * count * rows * naux * depth, bytes_accessed=2 * three_centre.size, transcendentals=10**4
+            flops=2 * count * rows * width * depth, bytes_accessed=2 * three_centre.size, transcendentals=10**4
         ),
     )(*[pltpu.with_memory_space_constraint(v, pltpu.HBM) for v in operands])
-    return results[0], results[1], results[2:]
-
-
-def partial_kernel(masks, received, layers, w_ref, held, *refs):
+
+
+def partial_kernel(masks, layers, first, has_arrived, w_ref, held, *refs):
+    arrived = refs[0] if has_arrived else None
+    out, scaled = refs[-2:]
     count = len(masks)
-    arrived = refs[: count if received else 0]
-    outs, scaled = refs[-1 - count : -1], refs[-1]
-    rows, naux = outs[0].shape
+    rows, width = out.shape[0] // count, out.shape[1]
     me, z, n_pair = lax.axis_index("pair"), lax.axis_index("tm"), lax.axis_size("pair")
     height = rows // layers
     for b, mask in enumerate(masks):
@@ -176,31 +174,50 @@
             row = owner if layers == 1 else jnp.bitwise_xor(z, part) * n_pair + owner
             old = pl.ds(pl.multiple_of(row * height, SUBLANES), height)
             scale_rows(scaled, pl.ds(b * rows + part * height, height), lambda cols: held[old, cols], w_ref)
-    tile = math.gcd(naux, TILE)
-    for n in range(naux // tile):
-        here = pl.ds(n * tile, tile)
-        multiply(scaled, held[here, :], here, outs, arrived)
-
-
-def partial_rows(held, weights, masks, dtypes, rows, layers, arrived=None):
-    naux, depth = held.shape
+    tile = math.gcd(width, TILE)
+    for n in range(width // tile):
+        multiply(scaled, held[pl.ds(first + n * tile, tile), :], pl.ds(n * tile, tile), out, arrived)
+
+
+def partial_rows(held, weights, masks, dtype, rows, layers, first, width, arrived=None):
+    _, depth = held.shape
     count = len(masks)
     vmem = pl.BlockSpec(memory_space=pltpu.VMEM)
-    operands = [weights, held] + (arrived or [])
-    return pl.pallas_call(
-        functools.partial(partial_kernel, masks, arrived is not None, layers),
+    operands = [pltpu.with_memory_space_constraint(v, pltpu.VMEM) for v in (weights, held)]
+    operands += [] if arrived is None else [arrived]
+    return pl.pallas_call(
+        functools.partial(partial_kernel, masks, layers, first, arrived is not None),
         in_specs=[vmem] * len(operands),
-        out_specs=[vmem] * count,
+        out_specs=vmem,
         scratch_shapes=[pltpu.VMEM((count * rows, depth), jnp.bfloat16)],
-        out_shape=[jax.ShapeDtypeStruct((rows, naux), t) for t in dtypes],
+        out_shape=jax.ShapeDtypeStruct((count * rows, width), dtype),
         name="partial",
         compiler_params=pltpu.CompilerParams(vmem_limit_bytes=16 * 2**20),
         cost_estimate=pl.CostEstimate(
-            flops=2 * count * rows * naux * depth,
-            bytes_accessed=2 * (naux + count * rows) * depth + 4 * count * rows * naux,
+            flops=2 * count * rows * width * depth,
+            bytes_accessed=2 * (width + count * rows) * depth + 4 * count * rows * width,
             transcendentals=0,
         ),
-    )(*[pltpu.with_memory_space_constraint(v, pltpu.VMEM) for v in operands[:2]], *operands[2:])
+    )(*operands)
+
+
+def pass_kernel(mine, other, out):
+    rows = out.shape[0]
+    out[...] = (mine[:rows].astype(jnp.float32) + other[:rows].astype(jnp.float32)).astype(out.dtype)
+
+
+def pass_on(mine, other, rows):
+    vmem = pl.BlockSpec(memory_space=pltpu.VMEM)
+    width = mine.shape[1]
+    return pl.pallas_call(
+        pass_kernel,
+        in_specs=[vmem] * 2,
+        out_specs=vmem,
+        out_shape=jax.ShapeDtypeStruct((rows, width), jnp.bfloat16),
+        name="pass_on",
+        compiler_params=pltpu.CompilerParams(vmem_limit_bytes=4 * 2**20),
+        cost_estimate=pl.CostEstimate(flops=10**8, bytes_accessed=8 * rows * width, transcendentals=0),
+    )(mine, other)
 
 
 def lay(root, first_layer, last_layer, plan, pieces, height):
@@ -244,49 +261,54 @@
     )(*values)
 
 
-def screen_kernel(n_terms, *refs):
+def screen_kernel(plan, n_terms, *refs):
     terms = refs[:n_terms]
     root, out, chi = refs[n_terms:]
-    value = terms[0][...].astype(jnp.float32)
-    for term in terms[1:]:
-        value += term[...].astype(jnp.float32)
-    chi[...] = value.astype(jnp.bfloat16)
+    rows = out.shape[0]
+    sums = {}
+    for term, (column, first) in zip(terms, plan):
+        value = term[first : first + rows].astype(jnp.float32)
+        sums[column] = value if column not in sums else sums[column] + value
+    for column, value in sums.items():
+        cols = pl.ds(column, value.shape[1])
+        high = value.astype(jnp.bfloat16)
+        chi[:rows, cols] = high
+        chi[rows:, cols] = (value - high.astype(jnp.float32)).astype(jnp.bfloat16)
     tile = math.gcd(out.shape[1], TILE)
     for n in range(out.shape[1] // tile):
         cols = pl.ds(n * tile, tile)
-        out[:, cols] = jnp.dot(chi[:, : root.shape[0]], root[:, cols], preferred_element_type=jnp.float32)
-
-
-def screen(terms, root):
-    rows, naux = terms[0].shape
-    vmem = pl.BlockSpec(memory_space=pltpu.VMEM)
-    return pl.pallas_call(
-        functools.partial(screen_kernel, len(terms)),
+        both = jnp.dot(chi[:, : root.shape[0]], root[:, cols], preferred_element_type=jnp.float32)
+        out[:, cols] = both[:rows] + both[rows:]
+
+
+def screen(terms, root, rows, naux):
+    vmem = pl.BlockSpec(memory_space=pltpu.VMEM)
+    return pl.pallas_call(
+        functools.partial(screen_kernel, [t[:2] for t in terms], len(terms)),
         in_specs=[vmem] * (len(terms) + 1),
         out_specs=[vmem] * 2,
         out_shape=[
             jax.ShapeDtypeStruct((rows, root.shape[1]), jnp.float32),
-            jax.ShapeDtypeStruct((rows, naux), jnp.bfloat16),
+            jax.ShapeDtypeStruct((2 * rows, naux), jnp.bfloat16),
         ],
         name="screen",
-        compiler_params=pltpu.CompilerParams(vmem_limit_bytes=8 * 2**20),
+        compiler_params=pltpu.CompilerParams(vmem_limit_bytes=12 * 2**20),
         cost_estimate=pl.CostEstimate(
-            flops=2 * rows * root.size, bytes_accessed=2 * root.size + 6 * rows * naux, transcendentals=0
+            flops=4 * rows * root.size, bytes_accessed=2 * root.size + 6 * rows * naux, transcendentals=0
         ),
-    )(*terms, root)
+    )(*[t[2] for t in terms], root)
 
 
 def finish_kernel(plan, layer, height, total, chi, *refs):
     pieces, (out, root, staged, sems) = refs[: len(plan)], refs[len(plan) :]
     lay(root, layer, layer + 1, plan, pieces, height)
-    depth = root.shape[0]
+    depth, rows = root.shape[0], total.shape[0]
     tile = math.gcd(out.shape[2], TILE)
     copies = []
     for n in range(out.shape[2] // tile):
         cols = pl.ds(n * tile, tile)
-        staged[:, cols] = total[:, cols] + jnp.dot(
-            chi[:, chi.shape[1] - depth :], root[:, cols], preferred_element_type=jnp.float32
-        )
+        both = jnp.dot(chi[:, chi.shape[1] - depth :], root[:, cols], preferred_element_type=jnp.float32)
+        staged[:, cols] = total[:, cols] + (both[:rows] + both[rows:])
         copies.append(pltpu.make_async_copy(staged.at[:, cols], out.at[0, :, cols], sems.at[n]))
         copies[-1].start()
     for copy in copies:
@@ -373,32 +395,61 @@
 def shards(layers, three_centre, root_coulomb, occ_depth, vir_energy, occ_block, vir_block):
     n_pair, n_tm = lax.axis_size("pair"), lax.axis_size("tm")
     height = root_coulomb.shape[0]
-    rows = three_centre.shape[0] // n_pair
+    naux = three_centre.shape[0]
+    rows = naux // n_pair
+    tables = (occ_depth, vir_energy, occ_block, vir_block)
     if layers == 1:
-        root = lax.all_gather(root_coulomb, AXES, axis=0, tiled=True)
-    else:
-        pieces = gather_root(root_coulomb)
-        root = collect(pieces, layers - 1, height, three_centre.shape[0])
-    halves = []
+        return plain(three_centre, root_coulomb, tables, rows)
+    pieces = gather_root(root_coulomb)
+    root = collect(pieces, layers - 1, height, naux)
+    x, y = 2, 4
+    half = naux // 2
+    jobs = {"a": ((x | y, x), 0), "b": ((x | y, y), half), "c": ((x, 0), half), "d": ((y, 0), 0)}
+    others = {}
+    for name, (masks, first) in jobs.items():
+        masks = tuple(m ^ 1 for m in masks)
+        if name == "a":
+            weights, held, part = first_rows(three_centre, *tables, masks, rows, layers, n_tm, first, half)
+        else:
+            part = partial_rows(held, weights, masks, jnp.bfloat16, rows, layers, first, half)
+        others[name] = swap(part, 1)
+    sums = {}
+    for name, (masks, first) in jobs.items():
+        dtype = jnp.bfloat16 if name in "ab" else jnp.float32
+        sums[name] = partial_rows(held, weights, masks, dtype, rows, layers, first, half, others[name])
+    one_x = swap(sums["a"], x)
+    one_y = swap(sums["b"], y)
+    send_y = pass_on(sums["d"], one_x, rows)
+    send_x = pass_on(sums["c"], one_y, rows)
+    two_y = swap(send_y, y)
+    two_x = swap(send_x, x)
+    terms = [
+        (0, rows, sums["d"]), (0, rows, one_x), (0, 0, two_y),
+        (half, rows, sums["c"]), (half, rows, one_y), (half, 0, two_x),
+    ]
+    total, chi = screen(terms, root, rows, naux)
+    return finish(total, chi, pieces, layers - 1, height)
+
+
+def plain(three_centre, root_coulomb, tables, rows):
+    n_pair, n_tm = lax.axis_size("pair"), lax.axis_size("tm")
+    naux = three_centre.shape[0]
+    root = lax.all_gather(root_coulomb, AXES, axis=0, tiled=True)
+    terms = []
     groups = chip_groups(n_pair, rows)
-    for g, group in enumerate(groups):
-        masks = [2 * m + 1 for m in group]
-        if g == 0:
-            weights, held, parts = first_rows(
-                three_centre, occ_depth, vir_energy, occ_block, vir_block, masks, rows, layers, n_tm
-            )
+    held = None
+    for group in groups:
+        masks = tuple(2 * m + 1 for m in group)
+        if held is None:
+            weights, held, part = first_rows(three_centre, *tables, masks, rows, 1, n_tm, 0, naux)
         else:
-            parts = partial_rows(held, weights, masks, [jnp.bfloat16] * len(group), rows, layers)
-        halves.append([swap(part, 1) for part in parts])
-    terms = []
-    for g, group in enumerate(groups):
-        dtypes = [jnp.bfloat16 if m else jnp.float32 for m in group]
-        sums = partial_rows(held, weights, [2 * m for m in group], dtypes, rows, layers, halves[g])
-        terms += [swap(part, 2 * m) if m else part for m, part in zip(group, sums)]
-    total, chi = screen(terms, root)
-    if layers == 1:
-        return total[None]
-    return finish(total, chi, pieces, layers - 1, height)
+            part = partial_rows(held, weights, masks, jnp.bfloat16, rows, 1, 0, naux)
+        other = swap(part, 1)
+        own = partial_rows(held, weights, tuple(2 * m for m in group), jnp.float32, rows, 1, 0, naux, other)
+        for i, m in enumerate(group):
+            value = own[i * rows : (i + 1) * rows]
+            terms.append((0, 0, swap(value.astype(jnp.bfloat16), 2 * m) if m else value))
+    return screen(terms, root, rows, naux)[0][None]
 
 
 def chip_groups(n_pair, rows):

time: 93.1 us -> 79.7 us (0.86)
  waiting for transfers between devices: 49.5 us -> 31.4 us
  starting transfers between devices: 25.4 us -> 27.7 us
  Pallas kernels: 16.7 us -> 18.9 us
    ppermute x23 -> x24, waiting for transfers between devices: 26.3 us -> 6.06 us  [swap(): return lax.ppermute(value, 'pair', [(p, p ^ mask) for p in range(n_pair)])]
    ppermute x23 -> x24, starting transfers between devices: 14.3 us -> 16.6 us  [swap(): return lax.ppermute(value, 'pair', [(p, p ^ mask) for p in range(n_pair)])]
    ppermute x8, waiting for transfers between devices: 23.2 us -> 25.4 us  [along(): return lax.ppermute(value, 'tm', moves)]
    pallas_call x5 -> x11, Pallas kernels: 15 us -> 16.9 us  [the longest x7 9.98 us: partial_rows(): pl.pallas_call(functools.partial(partial_kernel, masks, layers, first, ar...]
  transfers between devices with their start and end apart: 31 -> 32, of which waited for: 9 -> 8; matrix products, arithmetic and copies ran while one was open for 0% -> 0% of each run, Pallas kernels for 16% -> 22%
where the time goes in v2:
time: 79.7 us; the launch traced here: 79.5 us
  waiting for transfers between devices  31.4 us (39%)
  starting transfers between devices  27.7 us (35%)
  Pallas kernels  18.9 us (24%)
  local copies, waits for them, and re-layouts  0.95 us (1%)
    ppermute x8, waiting for transfers between devices, along(): return lax.ppermute(value, 'tm', moves)  25.4 us
    ppermute x24, starting transfers between devices, swap(): return lax.ppermute(value, 'pair', [(p, p ^ mask) for p in range(n_pair)])  16.6 us
    ppermute x8, starting transfers between devices, along(): return lax.ppermute(value, 'tm', moves)  11.1 us
    pallas_call x7, Pallas kernels, partial_rows(): pl.pallas_call(functools.partial(partial_kernel, masks, layers, first, ar...  9.98 us
    ppermute x24, waiting for transfers between devices, swap(): return lax.ppermute(value, 'pair', [(p, p ^ mask) for p in range(n_pair)])  6.06 us
    pallas_call x1, Pallas kernels, first_rows(): pl.pallas_call(functools.partial(first_kernel, taus, coef, layers, masks,...  5.14 us
    pallas_call x1, Pallas kernels, screen(): pl.pallas_call(functools.partial(screen_kernel, [t[:2] for t in terms], l...  1.72 us
    pallas_call x1, Pallas kernels, finish(): pl.pallas_call(functools.partial(finish_kernel, plan, layer, height), in_...  1.64 us
  transfers between devices with their start and end apart: 32, of which 8 were waited for; matrix products, arithmetic and copies ran while one was open for 0% of the time, Pallas kernels for 22%

profile of v2, /device:TPU:0, one launch (start us, length us, event | category | flops | bytes accessed | tf_op | source)
XLA Modules:
  0.0 79.5 jit_solution(8907446934678932402)
XLA Ops:
  0.0 0.9 %fusion = (bf16[48,768]{1,0:T(8,128)(2,1)S(1)}, bf16[48,768]{1,0:T(8,128)(2,1)S(1)}) fusion(bf16[48,1536]{1,0:T(8,128)(2,1)} %param.7), kind=kLoop, calls=%fused_computation.2 | loop fusion | bytes 294912 | tf_op jit(solution)/shard_map/slice | solution.py:385
  0.9 5.1 %collective-permute-start.21 = (bf16[48,768]{1,0:T(8,128)(2,1)S(1)}, bf16[48,768]{1,0:T(8,128)(2,1)S(1)}, u32[]{:S(2)}, u32[]{:S(2)}) collective-permute-start(bf16[48,768]{1,0:T(8,128)(2,1)S(1)} %get-tuple-element.15), channel_id=1, source_target_pairs={{0,3},{1,2},{2,1},{3,0},{4,7},{5,6},{6,5},{7,4},{8,11},{9,10},{10,... | collective-permute-start | bytes 221192 | tf_op jit(solution)/shard_map/ppermute | solution.py:347
  6.7 2.6 %collective-permute-start.10 = (bf16[48,1536]{1,0:T(8,128)(2,1)}, bf16[48,1536]{1,0:T(8,128)(2,1)S(1)}, u32[]{:S(2)}, u32[]{:S(2)}) collective-permute-start(bf16[48,1536]{1,0:T(8,128)(2,1)} %param.7), channel_id=1, source_target_pairs={{0,24},{4,28},{8,16},{12,20},{16,8},{20,12},{24,0},{28,4},{1,25},{... | collective-permute-start | bytes 442376 | tf_op jit(solution)/shard_map/ppermute | solution.py:343
  9.3 3.0 %collective-permute-done.20 = bf16[48,768]{1,0:T(8,128)(2,1)S(1)} collective-permute-done((bf16[48,768]{1,0:T(8,128)(2,1)S(1)}, bf16[48,768]{1,0:T(8,128)(2,1)S(1)}, u32[]{:S(2)}, u32[]{:S(2)}) %collective-permute-start.20) | collective-permute-done | bytes 73760 | tf_op jit(solution)/shard_map/ppermute | solution.py:347
  12.4 1.6 %collective-permute-start.9 = (bf16[48,1536]{1,0:T(8,128)(2,1)}, bf16[48,1536]{1,0:T(8,128)(2,1)S(1)}, u32[]{:S(2)}, u32[]{:S(2)}) collective-permute-start(bf16[48,1536]{1,0:T(8,128)(2,1)} %param.7), channel_id=1, source_target_pairs={{0,16},{4,20},{8,24},{12,28},{16,0},{20,4},{24,8},{28,12},{1,17},{... | collective-permute-start | bytes 442376 | tf_op jit(solution)/shard_map/ppermute | solution.py:343
  14.0 1.5 %collective-permute-start.8 = (bf16[48,1536]{1,0:T(8,128)(2,1)}, bf16[48,1536]{1,0:T(8,128)(2,1)S(1)}, u32[]{:S(2)}, u32[]{:S(2)}) collective-permute-start(bf16[48,1536]{1,0:T(8,128)(2,1)} %param.7), channel_id=1, source_target_pairs={{0,8},{4,12},{8,0},{12,4},{16,24},{20,28},{24,16},{28,20},{1,9},{5... | collective-permute-start | bytes 442376 | tf_op jit(solution)/shard_map/ppermute | solution.py:343
  16.5 5.1 %first.1 = (f32[8,256]{1,0:T(8,128)S(1)}, bf16[1536,2048]{1,0:T(8,128)(2,1)S(1)}, bf16[384,768]{1,0:T(8,128)(2,1)S(1)}) custom-call(s32[8]{0:T(128)} %occ_block.1, s32[8]{0:T(128)} %vir_block.1, f32[1,256]{1,0:T(1,128)} %bitcast.3, f32[1,1024]{1,0:T(1,128)} %bitcast.2, bf16[1536,2048]{1,0:T(8,128)(2,1)} %source.1), custom_call_target="tpu_custom_call" | custom-call | flops 1207959552 | bytes 6291456 | tf_op jit(solution)/shard_map/first/pallas_call | solution.py:143
  21.8 2.7 %collective-permute-start.27 = (bf16[192,768]{1,0:T(8,128)(2,1)S(1)}, bf16[192,768]{1,0:T(8,128)(2,1)S(1)}, u32[]{:S(2)}, u32[]{:S(2)}) collective-permute-start(bf16[192,768]{1,0:T(8,128)(2,1)S(1)} %pad_maximum_fusion.1.refs_8_.refs_4_), channel_id=1, source_target_pairs={{0,24},{4,28},{8,16},{12,20},{16,8},{20,12},{24,0},{28,4},{1,25},{... | collective-permute-start | bytes 884744 | tf_op jit(solution)/shard_map/ppermute | solution.py:343
  24.8 1.4 %partial.12 = bf16[384,768]{1,0:T(8,128)(2,1)S(1)} custom-call(f32[8,256]{1,0:T(8,128)S(1)} %get-tuple-element.10.w_ref, bf16[1536,2048]{1,0:T(8,128)(2,1)S(1)} %get-tuple-element.11.held), custom_call_target="tpu_custom_call" | custom-call | flops 1207959552 | bytes 5898240 | tf_op jit(solution)/shard_map/partial/pallas_call | solution.py:188
  26.3 0.7 collective-permute-done.23.refs_10_.refs_6_
  27.0 1.3 %collective-permute-start.12 = (bf16[192,768]{1,0:T(8,128)(2,1)S(1)}, bf16[192,768]{1,0:T(8,128)(2,1)S(1)}, u32[]{:S(2)}, u32[]{:S(2)}) collective-permute-start(bf16[192,768]{1,0:T(8,128)(2,1)S(1)} %pad_maximum_fusion.refs_0_), channel_id=1, source_target_pairs={{0,1},{1,0},{2,3},{3,2},{4,5},{5,4},{6,7},{7,6},{8,9},{9,8},{10,11... | collective-permute-start | bytes 884744 | tf_op jit(solution)/shard_map/ppermute | solution.py:347
  28.2 1.4 %partial.7 = bf16[384,768]{1,0:T(8,128)(2,1)S(1)} custom-call(f32[8,256]{1,0:T(8,128)S(1)} %get-tuple-element.10.w_ref, bf16[1536,2048]{1,0:T(8,128)(2,1)S(1)} %get-tuple-element.11.held), custom_call_target="tpu_custom_call" | custom-call | flops 1207959552 | bytes 5898240 | tf_op jit(solution)/shard_map/partial/pallas_call | solution.py:188
  29.7 1.4 %partial.10 = bf16[384,768]{1,0:T(8,128)(2,1)S(1)} custom-call(f32[8,256]{1,0:T(8,128)S(1)} %get-tuple-element.10.w_ref, bf16[1536,2048]{1,0:T(8,128)(2,1)S(1)} %get-tuple-element.11.held), custom_call_target="tpu_custom_call" | custom-call | flops 1207959552 | bytes 5898240 | tf_op jit(solution)/shard_map/partial/pallas_call | solution.py:188
  31.1 1.6 %collective-permute-done.27.refs_14_.refs_10_ = bf16[192,768]{1,0:T(8,128)(2,1)S(1)} collective-permute-done((bf16[192,768]{1,0:T(8,128)(2,1)S(1)}, bf16[192,768]{1,0:T(8,128)(2,1)S(1)}, u32[]{:S(2)}, u32[]{:S(2)}) %collective-permute-start.27) | collective-permute-done | bytes 294944 | tf_op jit(solution)/shard_map/ppermute | solution.py:343
  33.2 3.2 %collective-permute-done.12.refs_2_ = bf16[192,768]{1,0:T(8,128)(2,1)S(1)} collective-permute-done((bf16[192,768]{1,0:T(8,128)(2,1)S(1)}, bf16[192,768]{1,0:T(8,128)(2,1)S(1)}, u32[]{:S(2)}, u32[]{:S(2)}) %collective-permute-start.12) | collective-permute-done | bytes 294944 | tf_op jit(solution)/shard_map/ppermute | solution.py:347
  36.4 0.7 collective-permute-start.16
  37.2 1.4 %partial.9 = bf16[384,768]{1,0:T(8,128)(2,1)S(1)} custom-call(f32[8,256]{1,0:T(8,128)S(1)} %get-tuple-element.10.w_ref, bf16[1536,2048]{1,0:T(8,128)(2,1)S(1)} %get-tuple-element.11.held, bf16[384,768]{1,0:T(8,128)(2,1)S(1)} %collective-permute-done.1.refs_0_), custom_call_target="tpu_custom_call" | custom-call | flops 1207959552 | bytes 5898240 | tf_op jit(solution)/shard_map/partial/pallas_call | solution.py:188
  38.6 1.3 %collective-permute-start.2 = (bf16[384,768]{1,0:T(8,128)(2,1)S(1)}, bf16[384,768]{1,0:T(8,128)(2,1)S(1)}, u32[]{:S(2)}, u32[]{:S(2)}) collective-permute-start(bf16[384,768]{1,0:T(8,128)(2,1)S(1)} %partial.9), channel_id=1, source_target_pairs={{0,8},{4,12},{8,0},{12,4},{16,24},{20,28},{24,16},{28,20},{1,9},{5... | collective-permute-start | bytes 1769480 | tf_op jit(solution)/shard_map/ppermute | solution.py:343
  39.9 1.4 %partial.13 = bf16[384,768]{1,0:T(8,128)(2,1)S(1)} custom-call(f32[8,256]{1,0:T(8,128)S(1)} %get-tuple-element.10.w_ref, bf16[1536,2048]{1,0:T(8,128)(2,1)S(1)} %get-tuple-element.11.held, bf16[384,768]{1,0:T(8,128)(2,1)S(1)} %collective-permute-done.5.refs_0_), custom_call_target="tpu_custom_call" | custom-call | flops 1207959552 | bytes 5898240 | tf_op jit(solution)/shard_map/partial/pallas_call | solution.py:188
  41.9 0.7 collective-permute-start.14
  42.6 1.3 %collective-permute-start.17 = (bf16[192,768]{1,0:T(8,128)(2,1)S(1)}, bf16[192,768]{1,0:T(8,128)(2,1)S(1)}, u32[]{:S(2)}, u32[]{:S(2)}) collective-permute-start(bf16[192,768]{1,0:T(8,128)(2,1)S(1)} %collective-permute-done.16.refs_0_), channel_id=1, source_target_pairs={{1,0},{2,3},{5,4},{6,7},{9,8},{10,11},{13,12},{14,15},{17,16},{18,... | collective-permute-start | bytes 884744 | tf_op jit(solution)/shard_map/ppermute | solution.py:347
  44.6 16.0 %collective-permute-done.17.refs_6_ = bf16[192,768]{1,0:T(8,128)(2,1)S(1)} collective-permute-done((bf16[192,768]{1,0:T(8,128)(2,1)S(1)}, bf16[192,768]{1,0:T(8,128)(2,1)S(1)}, u32[]{:S(2)}, u32[]{:S(2)}) %collective-permute-start.17) | collective-permute-done | bytes 294944 | tf_op jit(solution)/shard_map/ppermute | solution.py:347
  60.6 1.5 %collective-permute-start.30 = (bf16[192,768]{1,0:T(8,128)(2,1)S(1)}, bf16[192,768]{1,0:T(8,128)(2,1)S(1)}, u32[]{:S(2)}, u32[]{:S(2)}) collective-permute-start(bf16[192,768]{1,0:T(8,128)(2,1)S(1)} %collective-permute-done.14.refs_4_), channel_id=1, source_target_pairs={{1,0},{2,3},{5,4},{6,7},{9,8},{10,11},{13,12},{14,15},{17,16},{18,... | collective-permute-start | bytes 884744 | tf_op jit(solution)/shard_map/ppermute | solution.py:347
  62.1 1.4 %partial.8.mine.refs_0_ = f32[384,768]{1,0:T(8,128)S(1)} custom-call(f32[8,256]{1,0:T(8,128)S(1)} %get-tuple-element.10.w_ref, bf16[1536,2048]{1,0:T(8,128)(2,1)S(1)} %get-tuple-element.11.held, bf16[384,768]{1,0:T(8,128)(2,1)S(1)} %collective-permute-done.refs_0_), custom_call_target="tpu_custom_call" | custom-call | flops 1207959552 | bytes 5898240 | tf_op jit(solution)/shard_map/partial/pallas_call | solution.py:188
  64.1 1.4 %partial.11.mine.refs_3_ = f32[384,768]{1,0:T(8,128)S(1)} custom-call(f32[8,256]{1,0:T(8,128)S(1)} %get-tuple-element.10.w_ref, bf16[1536,2048]{1,0:T(8,128)(2,1)S(1)} %get-tuple-element.11.held, bf16[384,768]{1,0:T(8,128)(2,1)S(1)} %collective-permute-done.4.refs_0_), custom_call_target="tpu_custom_call" | custom-call | flops 1207959552 | bytes 5898240 | tf_op jit(solution)/shard_map/partial/pallas_call | solution.py:188
  65.7 1.6 %collective-permute-start.3 = (bf16[192,768]{1,0:T(8,128)(2,1)S(1)}, bf16[192,768]{1,0:T(8,128)(2,1)S(1)}, u32[]{:S(2)}, u32[]{:S(2)}) collective-permute-start(bf16[192,768]{1,0:T(8,128)(2,1)S(1)} %pass_on.2), channel_id=1, source_target_pairs={{0,16},{4,20},{8,24},{12,28},{16,0},{20,4},{24,8},{28,12},{1,17},{... | collective-permute-start | bytes 884744 | tf_op jit(solution)/shard_map/ppermute | solution.py:343
  67.3 1.5 %collective-permute-start.7 = (bf16[192,768]{1,0:T(8,128)(2,1)S(1)}, bf16[192,768]{1,0:T(8,128)(2,1)S(1)}, u32[]{:S(2)}, u32[]{:S(2)}) collective-permute-start(bf16[192,768]{1,0:T(8,128)(2,1)S(1)} %pass_on.3), channel_id=1, source_target_pairs={{0,8},{4,12},{8,0},{12,4},{16,24},{20,28},{24,16},{28,20},{1,9},{5... | collective-permute-start | bytes 884744 | tf_op jit(solution)/shard_map/ppermute | solution.py:343
  68.8 3.2 %collective-permute-done.30.refs_2_ = bf16[192,768]{1,0:T(8,128)(2,1)S(1)} collective-permute-done((bf16[192,768]{1,0:T(8,128)(2,1)S(1)}, bf16[192,768]{1,0:T(8,128)(2,1)S(1)}, u32[]{:S(2)}, u32[]{:S(2)}) %collective-permute-start.30) | collective-permute-done | bytes 294944 | tf_op jit(solution)/shard_map/ppermute | solution.py:347
  72.2 2.5 %collective-permute-done.3.refs_2_ = bf16[192,768]{1,0:T(8,128)(2,1)S(1)} collective-permute-done((bf16[192,768]{1,0:T(8,128)(2,1)S(1)}, bf16[192,768]{1,0:T(8,128)(2,1)S(1)}, u32[]{:S(2)}, u32[]{:S(2)}) %collective-permute-start.3) | collective-permute-done | bytes 294944 | tf_op jit(solution)/shard_map/ppermute | solution.py:343
  74.7 1.2 %collective-permute-done.7.refs_5_ = bf16[192,768]{1,0:T(8,128)(2,1)S(1)} collective-permute-done((bf16[192,768]{1,0:T(8,128)(2,1)S(1)}, bf16[192,768]{1,0:T(8,128)(2,1)S(1)}, u32[]{:S(2)}, u32[]{:S(2)}) %collective-permute-start.7) | collective-permute-done | bytes 294944 | tf_op jit(solution)/shard_map/ppermute | solution.py:343
  75.9 1.7 %screen.1 = (f32[192,1536]{1,0:T(8,128)S(1)}, bf16[384,1536]{1,0:T(8,128)(2,1)S(1)}) custom-call(f32[384,768]{1,0:T(8,128)S(1)} %partial.8.mine.refs_0_, bf16[384,768]{1,0:T(8,128)(2,1)S(1)} %collective-permute-done.2.other.refs_1_, bf16[192,768]{1,0:T(8,128)(2,1)S(1)} %collective-permute-done.3.refs_2_, f32[384,768]{1,0:T(8,128)S(1)} %partial.11.mine.refs_3_, ...), custom_call_target="tpu_custom_call" | custom-call | flops 1358954496 | bytes 5308416 | tf_op jit(solution)/shard_map/screen/pallas_call | solution.py:286
  77.7 1.6 %finish.1 = f32[1,192,1536]{2,1,0:T(8,128)} custom-call(f32[192,1536]{1,0:T(8,128)S(1)} %get-tuple-element.13.total, bf16[384,1536]{1,0:T(8,128)(2,1)S(1)} %get-tuple-element.14.chi, bf16[192,768]{1,0:T(8,128)(2,1)S(1)} %collective-permute-done.16.refs_0_, bf16[192,768]{1,0:T(8,128)(2,1)S(1)} %collective-permute-done.29.refs_1_, ...), custom_call_target="tpu_custom_call" | custom-call | flops 226492416 | bytes 3538944 | tf_op jit(solution)/shard_map/finish/pallas_call | solution.py:323
  (51 shorter events, 5.0 us)
Async XLA Ops:
  0.9 8.4 %collective-permute-start.21 = (bf16[48,768]{1,0:T(8,128)(2,1)S(1)}, bf16[48,768]{1,0:T(8,128)(2,1)S(1)}, u32[]{:S(2)}, u32[]{:S(2)}) collective-permute-start(bf16[48,768]{1,0:T(8,128)(2,1)S(1)} %get-tuple-element.15), channel_id=1, source_target_pairs={{0,3},{1,2},{2,1},{3,0},{4,7},{5,6},{6,5},{7,4},{8,11},{9,10},{10,... | collective-permute-start | bytes 221192 | tf_op jit(solution)/shard_map/ppermute | solution.py:347
  6.1 6.2 %collective-permute-start.20 = (bf16[48,768]{1,0:T(8,128)(2,1)S(1)}, bf16[48,768]{1,0:T(8,128)(2,1)S(1)}, u32[]{:S(2)}, u32[]{:S(2)}) collective-permute-start(bf16[48,768]{1,0:T(8,128)(2,1)S(1)} %get-tuple-element.15), channel_id=1, source_target_pairs={{0,2},{1,3},{2,0},{3,1},{4,6},{5,7},{6,4},{7,5},{8,10},{9,11},{10,... | collective-permute-start | bytes 221192 | tf_op jit(solution)/shard_map/ppermute | solution.py:347
  6.1 6.2 %collective-permute-start.19 = (bf16[48,768]{1,0:T(8,128)(2,1)S(1)}, bf16[48,768]{1,0:T(8,128)(2,1)S(1)}, u32[]{:S(2)}, u32[]{:S(2)}) collective-permute-start(bf16[48,768]{1,0:T(8,128)(2,1)S(1)} %get-tuple-element.15), channel_id=1, source_target_pairs={{0,1},{1,0},{2,3},{3,2},{4,5},{5,4},{6,7},{7,6},{8,9},{9,8},{10,11... | collective-permute-start | bytes 221192 | tf_op jit(solution)/shard_map/ppermute | solution.py:347
  6.7 9.3 %collective-permute-start.10 = (bf16[48,1536]{1,0:T(8,128)(2,1)}, bf16[48,1536]{1,0:T(8,128)(2,1)S(1)}, u32[]{:S(2)}, u32[]{:S(2)}) collective-permute-start(bf16[48,1536]{1,0:T(8,128)(2,1)} %param.7), channel_id=1, source_target_pairs={{0,24},{4,28},{8,16},{12,20},{16,8},{20,12},{24,0},{28,4},{1,25},{... | collective-permute-start | bytes 442376 | tf_op jit(solution)/shard_map/ppermute | solution.py:343
  12.3 12.2 %collective-permute-start.22 = (bf16[192,768]{1,0:T(8,128)(2,1)S(1)}, bf16[192,768]{1,0:T(8,128)(2,1)S(1)}, u32[]{:S(2)}, u32[]{:S(2)}) collective-permute-start(bf16[192,768]{1,0:T(8,128)(2,1)S(1)} %pad_maximum_fusion.1.refs_8_.refs_4_), channel_id=1, source_target_pairs={{0,4},{4,0},{8,12},{12,8},{16,20},{20,16},{24,28},{28,24},{1,5},{5... | collective-permute-start | bytes 884744 | tf_op jit(solution)/shard_map/ppermute | solution.py:343
  12.4 9.3 %collective-permute-start.9 = (bf16[48,1536]{1,0:T(8,128)(2,1)}, bf16[48,1536]{1,0:T(8,128)(2,1)S(1)}, u32[]{:S(2)}, u32[]{:S(2)}) collective-permute-start(bf16[48,1536]{1,0:T(8,128)(2,1)} %param.7), channel_id=1, source_target_pairs={{0,16},{4,20},{8,24},{12,28},{16,0},{20,4},{24,8},{28,12},{1,17},{... | collective-permute-start | bytes 442376 | tf_op jit(solution)/shard_map/ppermute | solution.py:343
  14.0 7.8 %collective-permute-start.8 = (bf16[48,1536]{1,0:T(8,128)(2,1)}, bf16[48,1536]{1,0:T(8,128)(2,1)S(1)}, u32[]{:S(2)}, u32[]{:S(2)}) collective-permute-start(bf16[48,1536]{1,0:T(8,128)(2,1)} %param.7), channel_id=1, source_target_pairs={{0,8},{4,12},{8,0},{12,4},{16,24},{20,28},{24,16},{28,20},{1,9},{5... | collective-permute-start | bytes 442376 | tf_op jit(solution)/shard_map/ppermute | solution.py:343
  15.5 11.5 %collective-permute-start.23 = (bf16[192,768]{1,0:T(8,128)(2,1)S(1)}, bf16[192,768]{1,0:T(8,128)(2,1)S(1)}, u32[]{:S(2)}, u32[]{:S(2)}) collective-permute-start(bf16[192,768]{1,0:T(8,128)(2,1)S(1)} %pad_maximum_fusion.1.refs_8_.refs_4_), channel_id=1, source_target_pairs={{0,8},{4,12},{8,0},{12,4},{16,24},{20,28},{24,16},{28,20},{1,9},{5... | collective-permute-start | bytes 884744 | tf_op jit(solution)/shard_map/ppermute | solution.py:343
  16.0 11.0 %collective-permute-start.25 = (bf16[192,768]{1,0:T(8,128)(2,1)S(1)}, bf16[192,768]{1,0:T(8,128)(2,1)S(1)}, u32[]{:S(2)}, u32[]{:S(2)}) collective-permute-start(bf16[192,768]{1,0:T(8,128)(2,1)S(1)} %pad_maximum_fusion.1.refs_8_.refs_4_), channel_id=1, source_target_pairs={{0,16},{4,20},{8,24},{12,28},{16,0},{20,4},{24,8},{28,12},{1,17},{... | collective-permute-start | bytes 884744 | tf_op jit(solution)/shard_map/ppermute | solution.py:343
  21.7 15.4 %collective-permute-start.1 = (bf16[384,768]{1,0:T(8,128)(2,1)S(1)}, bf16[384,768]{1,0:T(8,128)(2,1)S(1)}, u32[]{:S(2)}, u32[]{:S(2)}) collective-permute-start(bf16[384,768]{1,0:T(8,128)(2,1)S(1)} %get-tuple-element.12), channel_id=1, source_target_pairs={{0,4},{4,0},{8,12},{12,8},{16,20},{20,16},{24,28},{28,24},{1,5},{5... | collective-permute-start | bytes 1769480 | tf_op jit(solution)/shard_map/ppermute | solution.py:343
  21.8 10.9 %collective-permute-start.27 = (bf16[192,768]{1,0:T(8,128)(2,1)S(1)}, bf16[192,768]{1,0:T(8,128)(2,1)S(1)}, u32[]{:S(2)}, u32[]{:S(2)}) collective-permute-start(bf16[192,768]{1,0:T(8,128)(2,1)S(1)} %pad_maximum_fusion.1.refs_8_.refs_4_), channel_id=1, source_target_pairs={{0,24},{4,28},{8,16},{12,20},{16,8},{20,12},{24,0},{28,4},{1,25},{... | collective-permute-start | bytes 884744 | tf_op jit(solution)/shard_map/ppermute | solution.py:343
  24.6 8.1 %collective-permute-start.11 = (bf16[192,768]{1,0:T(8,128)(2,1)S(1)}, bf16[192,768]{1,0:T(8,128)(2,1)S(1)}, u32[]{:S(2)}, u32[]{:S(2)}) collective-permute-start(bf16[192,768]{1,0:T(8,128)(2,1)S(1)} %pad_maximum_fusion.refs_0_), channel_id=1, source_target_pairs={{0,4},{4,0},{8,12},{12,8},{16,20},{20,16},{24,28},{28,24},{1,5},{5... | collective-permute-start | bytes 884744 | tf_op jit(solution)/shard_map/ppermute | solution.py:343
  27.0 11.6 %collective-permute-start.5 = (bf16[384,768]{1,0:T(8,128)(2,1)S(1)}, bf16[384,768]{1,0:T(8,128)(2,1)S(1)}, u32[]{:S(2)}, u32[]{:S(2)}) collective-permute-start(bf16[384,768]{1,0:T(8,128)(2,1)S(1)} %partial.12), channel_id=1, source_target_pairs={{0,4},{4,0},{8,12},{12,8},{16,20},{20,16},{24,28},{28,24},{1,5},{5... | collective-permute-start | bytes 1769480 | tf_op jit(solution)/shard_map/ppermute | solution.py:343
  27.0 9.4 %collective-permute-start.12 = (bf16[192,768]{1,0:T(8,128)(2,1)S(1)}, bf16[192,768]{1,0:T(8,128)(2,1)S(1)}, u32[]{:S(2)}, u32[]{:S(2)}) collective-permute-start(bf16[192,768]{1,0:T(8,128)(2,1)S(1)} %pad_maximum_fusion.refs_0_), channel_id=1, source_target_pairs={{0,1},{1,0},{2,3},{3,2},{4,5},{5,4},{6,7},{7,6},{8,9},{9,8},{10,11... | collective-permute-start | bytes 884744 | tf_op jit(solution)/shard_map/ppermute | solution.py:347
  32.7 9.2 %collective-permute-start = (bf16[384,768]{1,0:T(8,128)(2,1)S(1)}, bf16[384,768]{1,0:T(8,128)(2,1)S(1)}, u32[]{:S(2)}, u32[]{:S(2)}) collective-permute-start(bf16[384,768]{1,0:T(8,128)(2,1)S(1)} %partial.7), channel_id=1, source_target_pairs={{0,4},{4,0},{8,12},{12,8},{16,20},{20,16},{24,28},{28,24},{1,5},{5... | collective-permute-start | bytes 1769480 | tf_op jit(solution)/shard_map/ppermute | solution.py:343
  32.7 9.2 %collective-permute-start.4 = (bf16[384,768]{1,0:T(8,128)(2,1)S(1)}, bf16[384,768]{1,0:T(8,128)(2,1)S(1)}, u32[]{:S(2)}, u32[]{:S(2)}) collective-permute-start(bf16[384,768]{1,0:T(8,128)(2,1)S(1)} %partial.10), channel_id=1, source_target_pairs={{0,4},{4,0},{8,12},{12,8},{16,20},{20,16},{24,28},{28,24},{1,5},{5... | collective-permute-start | bytes 1769480 | tf_op jit(solution)/shard_map/ppermute | solution.py:343
  36.4 5.0 %collective-permute-start.16 = (bf16[192,768]{1,0:T(8,128)(2,1)S(1)}, bf16[192,768]{1,0:T(8,128)(2,1)S(1)}, u32[]{:S(2)}, u32[]{:S(2)}) collective-permute-start(bf16[192,768]{1,0:T(8,128)(2,1)S(1)} %pad_maximum_fusion.refs_0_), channel_id=1, source_target_pairs={{1,2},{2,1},{5,6},{6,5},{9,10},{10,9},{13,14},{14,13},{17,18},{18,... | collective-permute-start | bytes 884744 | tf_op jit(solution)/shard_map/ppermute | solution.py:347
  37.1 5.5 %collective-permute-start.24 = (bf16[192,768]{1,0:T(8,128)(2,1)S(1)}, bf16[192,768]{1,0:T(8,128)(2,1)S(1)}, u32[]{:S(2)}, u32[]{:S(2)}) collective-permute-start(bf16[192,768]{1,0:T(8,128)(2,1)S(1)} %collective-permute-done.23.refs_10_.refs_6_), channel_id=1, source_target_pairs={{0,4},{4,0},{8,12},{12,8},{16,20},{20,16},{24,28},{28,24},{1,5},{5... | collective-permute-start | bytes 884744 | tf_op jit(solution)/shard_map/ppermute | solution.py:343
  38.6 22.0 %collective-permute-start.2 = (bf16[384,768]{1,0:T(8,128)(2,1)S(1)}, bf16[384,768]{1,0:T(8,128)(2,1)S(1)}, u32[]{:S(2)}, u32[]{:S(2)}) collective-permute-start(bf16[384,768]{1,0:T(8,128)(2,1)S(1)} %partial.9), channel_id=1, source_target_pairs={{0,8},{4,12},{8,0},{12,4},{16,24},{20,28},{24,16},{28,20},{1,9},{5... | collective-permute-start | bytes 1769480 | tf_op jit(solution)/shard_map/ppermute | solution.py:343
  41.4 22.1 %collective-permute-start.6 = (bf16[384,768]{1,0:T(8,128)(2,1)S(1)}, bf16[384,768]{1,0:T(8,128)(2,1)S(1)}, u32[]{:S(2)}, u32[]{:S(2)}) collective-permute-start(bf16[384,768]{1,0:T(8,128)(2,1)S(1)} %partial.13), channel_id=1, source_target_pairs={{0,16},{4,20},{8,24},{12,28},{16,0},{20,4},{24,8},{28,12},{1,17},{... | collective-permute-start | bytes 1769480 | tf_op jit(solution)/shard_map/ppermute | solution.py:343
  41.9 2.0 %collective-permute-start.26 = (bf16[192,768]{1,0:T(8,128)(2,1)S(1)}, bf16[192,768]{1,0:T(8,128)(2,1)S(1)}, u32[]{:S(2)}, u32[]{:S(2)}) collective-permute-start(bf16[192,768]{1,0:T(8,128)(2,1)S(1)} %collective-permute-done.25.refs_12_.refs_8_), channel_id=1, source_target_pairs={{0,4},{4,0},{8,12},{12,8},{16,20},{20,16},{24,28},{28,24},{1,5},{5... | collective-permute-start | bytes 884744 | tf_op jit(solution)/shard_map/ppermute | solution.py:343
  41.9 2.6 %collective-permute-start.14 = (bf16[192,768]{1,0:T(8,128)(2,1)S(1)}, bf16[192,768]{1,0:T(8,128)(2,1)S(1)}, u32[]{:S(2)}, u32[]{:S(2)}) collective-permute-start(bf16[192,768]{1,0:T(8,128)(2,1)S(1)} %collective-permute-done.12.refs_2_), channel_id=1, source_target_pairs={{1,2},{2,1},{5,6},{6,5},{9,10},{10,9},{13,14},{14,13},{17,18},{18,... | collective-permute-start | bytes 884744 | tf_op jit(solution)/shard_map/ppermute | solution.py:347
  42.6 18.0 %collective-permute-start.17 = (bf16[192,768]{1,0:T(8,128)(2,1)S(1)}, bf16[192,768]{1,0:T(8,128)(2,1)S(1)}, u32[]{:S(2)}, u32[]{:S(2)}) collective-permute-start(bf16[192,768]{1,0:T(8,128)(2,1)S(1)} %collective-permute-done.16.refs_0_), channel_id=1, source_target_pairs={{1,0},{2,3},{5,4},{6,7},{9,8},{10,11},{13,12},{14,15},{17,16},{18,... | collective-permute-start | bytes 884744 | tf_op jit(solution)/shard_map/ppermute | solution.py:347
  43.9 21.7 %collective-permute-start.28 = (bf16[192,768]{1,0:T(8,128)(2,1)S(1)}, bf16[192,768]{1,0:T(8,128)(2,1)S(1)}, u32[]{:S(2)}, u32[]{:S(2)}) collective-permute-start(bf16[192,768]{1,0:T(8,128)(2,1)S(1)} %collective-permute-done.27.refs_14_.refs_10_), channel_id=1, source_target_pairs={{0,4},{4,0},{8,12},{12,8},{16,20},{20,16},{24,28},{28,24},{1,5},{5... | collective-permute-start | bytes 884744 | tf_op jit(solution)/shard_map/ppermute | solution.py:343
  44.5 22.7 %collective-permute-start.13 = (bf16[192,768]{1,0:T(8,128)(2,1)S(1)}, bf16[192,768]{1,0:T(8,128)(2,1)S(1)}, u32[]{:S(2)}, u32[]{:S(2)}) collective-permute-start(bf16[192,768]{1,0:T(8,128)(2,1)S(1)} %collective-permute-done.12.refs_2_), channel_id=1, source_target_pairs={{0,4},{4,0},{8,12},{12,8},{16,20},{20,16},{24,28},{28,24},{1,5},{5... | collective-permute-start | bytes 884744 | tf_op jit(solution)/shard_map/ppermute | solution.py:343
  60.6 8.1 %collective-permute-start.15 = (bf16[192,768]{1,0:T(8,128)(2,1)S(1)}, bf16[192,768]{1,0:T(8,128)(2,1)S(1)}, u32[]{:S(2)}, u32[]{:S(2)}) collective-permute-start(bf16[192,768]{1,0:T(8,128)(2,1)S(1)} %collective-permute-done.14.refs_4_), channel_id=1, source_target_pairs={{0,4},{4,0},{8,12},{12,8},{16,20},{20,16},{24,28},{28,24},{1,5},{5... | collective-permute-start | bytes 884744 | tf_op jit(solution)/shard_map/ppermute | solution.py:343
  60.6 11.3 %collective-permute-start.30 = (bf16[192,768]{1,0:T(8,128)(2,1)S(1)}, bf16[192,768]{1,0:T(8,128)(2,1)S(1)}, u32[]{:S(2)}, u32[]{:S(2)}) collective-permute-start(bf16[192,768]{1,0:T(8,128)(2,1)S(1)} %collective-permute-done.14.refs_4_), channel_id=1, source_target_pairs={{1,0},{2,3},{5,4},{6,7},{9,8},{10,11},{13,12},{14,15},{17,16},{18,... | collective-permute-start | bytes 884744 | tf_op jit(solution)/shard_map/ppermute | solution.py:347
  63.5 8.4 %collective-permute-start.18 = (bf16[192,768]{1,0:T(8,128)(2,1)S(1)}, bf16[192,768]{1,0:T(8,128)(2,1)S(1)}, u32[]{:S(2)}, u32[]{:S(2)}) collective-permute-start(bf16[192,768]{1,0:T(8,128)(2,1)S(1)} %collective-permute-done.17.refs_6_), channel_id=1, source_target_pairs={{0,4},{4,0},{8,12},{12,8},{16,20},{20,16},{24,28},{28,24},{1,5},{5... | collective-permute-start | bytes 884744 | tf_op jit(solution)/shard_map/ppermute | solution.py:343
  65.7 9.0 %collective-permute-start.3 = (bf16[192,768]{1,0:T(8,128)(2,1)S(1)}, bf16[192,768]{1,0:T(8,128)(2,1)S(1)}, u32[]{:S(2)}, u32[]{:S(2)}) collective-permute-start(bf16[192,768]{1,0:T(8,128)(2,1)S(1)} %pass_on.2), channel_id=1, source_target_pairs={{0,16},{4,20},{8,24},{12,28},{16,0},{20,4},{24,8},{28,12},{1,17},{... | collective-permute-start | bytes 884744 | tf_op jit(solution)/shard_map/ppermute | solution.py:343
  67.3 8.6 %collective-permute-start.7 = (bf16[192,768]{1,0:T(8,128)(2,1)S(1)}, bf16[192,768]{1,0:T(8,128)(2,1)S(1)}, u32[]{:S(2)}, u32[]{:S(2)}) collective-permute-start(bf16[192,768]{1,0:T(8,128)(2,1)S(1)} %pass_on.3), channel_id=1, source_target_pairs={{0,8},{4,12},{8,0},{12,4},{16,24},{20,28},{24,16},{28,20},{1,9},{5... | collective-permute-start | bytes 884744 | tf_op jit(solution)/shard_map/ppermute | solution.py:343
  68.8 8.9 %collective-permute-start.29 = (bf16[192,768]{1,0:T(8,128)(2,1)S(1)}, bf16[192,768]{1,0:T(8,128)(2,1)S(1)}, u32[]{:S(2)}, u32[]{:S(2)}) collective-permute-start(bf16[192,768]{1,0:T(8,128)(2,1)S(1)} %collective-permute-done.16.refs_0_), channel_id=1, source_target_pairs={{0,4},{4,0},{8,12},{12,8},{16,20},{20,16},{24,28},{28,24},{1,5},{5... | collective-permute-start | bytes 884744 | tf_op jit(solution)/shard_map/ppermute | solution.py:343
  71.9 5.7 %collective-permute-start.31 = (bf16[192,768]{1,0:T(8,128)(2,1)S(1)}, bf16[192,768]{1,0:T(8,128)(2,1)S(1)}, u32[]{:S(2)}, u32[]{:S(2)}) collective-permute-start(bf16[192,768]{1,0:T(8,128)(2,1)S(1)} %collective-permute-done.30.refs_2_), channel_id=1, source_target_pairs={{0,4},{4,0},{8,12},{12,8},{16,20},{20,16},{24,28},{28,24},{1,5},{5... | collective-permute-start | bytes 884744 | tf_op jit(solution)/shard_map/ppermute | solution.py:343

commit v3 on v2

--- a/solution.py
+++ b/solution.py
@@ -221,25 +221,18 @@
 
 
 def lay(root, first_layer, last_layer, plan, pieces, height):
-    me, z, n_pair = lax.axis_index("pair"), lax.axis_index("tm"), lax.axis_size("pair")
-    for piece, (column, needed, blocks) in zip(pieces, plan):
+    me, n_pair = lax.axis_index("pair"), lax.axis_size("pair")
+    for piece, (column, blocks) in zip(pieces, plan):
         cols = pl.ds(column, piece.shape[1])
-
-        def move():
-            for i, (mask, layer) in enumerate(blocks):
-                if first_layer <= layer < last_layer:
-                    target = (jnp.bitwise_xor(me, mask) + (layer - first_layer) * n_pair) * height
-                    root[pl.ds(pl.multiple_of(target, SUBLANES), height), cols] = piece[i * height : (i + 1) * height, :]
-
-        if needed is None:
-            move()
-        else:
-            pl.when(needed(z))(move)
+        for i, (mask, layer) in enumerate(blocks):
+            if first_layer <= layer < last_layer:
+                target = (jnp.bitwise_xor(me, mask) + (layer - first_layer) * n_pair) * height
+                root[pl.ds(pl.multiple_of(target, SUBLANES), height), cols] = piece[i * height : (i + 1) * height, :]
 
 
 def choose(pieces, first_layer, last_layer):
-    kept = [p for p in pieces if any(first_layer <= layer < last_layer for _, layer in p[2])]
-    return [p[:3] for p in kept], [p[3] for p in kept]
+    kept = [p for p in pieces if any(first_layer <= layer < last_layer for _, layer in p[1])]
+    return [p[:2] for p in kept], [p[2] for p in kept]
 
 
 def collect_kernel(plan, last_layer, height, *refs):
@@ -343,16 +336,9 @@
     return lax.ppermute(value, "pair", [(p, p ^ mask) for p in range(n_pair)])
 
 
-def along(value, moves):
-    return lax.ppermute(value, "tm", moves)
-
-
-def is_inner(z):
-    return jnp.logical_or(z == 1, z == 2)
-
-
-def is_outer(z):
-    return jnp.logical_or(z == 0, z == 3)
+def along(value, layer):
+    n_tm = lax.axis_size("tm")
+    return lax.ppermute(value, "tm", [(z, z ^ layer) for z in range(n_tm)])
 
 
 def gather_root(root_coulomb):
@@ -360,35 +346,23 @@
     masks = [2 * m for m in range(n_pair // 2)]
     near = [root_coulomb] + [swap(root_coulomb, m) for m in masks[1:]]
     plane = jnp.concatenate([rows[:, SPLIT:] for rows in near], axis=0)
-    middle, outward = [(1, 2), (2, 1)], [(1, 0), (2, 3)]
-    first = along(plane, [(z, z ^ 1) for z in range(n_tm)])
-    second = along(plane, middle)
-    inner = along(first, middle)
-    outer = along(second, outward)
-    last = along(inner, outward)
+    layers = range(n_tm)
     pieces = []
 
-    def both(column, needed, blocks, value):
-        pieces.append((column, needed, blocks, value))
-        pieces.append((column, needed, [(m ^ 1, layer) for m, layer in blocks], swap(value, 1)))
-
-    for value, layer, needed in (
-        (plane, 0, None),
-        (first, 1, None),
-        (second, 3, is_inner),
-        (inner, 2, is_inner),
-        (outer, 2, is_outer),
-        (last, 3, is_outer),
-    ):
-        both(SPLIT, needed, [(m, layer) for m in masks], value)
+    def both(column, blocks, value):
+        pieces.append((column, blocks, value))
+        pieces.append((column, [(m ^ 1, layer) for m, layer in blocks], swap(value, 1)))
+
+    for layer in layers:
+        value = along(plane, layer) if layer else plane
+        both(SPLIT, [(m, layer) for m in masks], value)
     if SPLIT:
         tall = root_coulomb[:, :SPLIT]
-        layers = range(n_tm)
-        far = [tall] + [along(tall, [(z, z ^ m) for z in layers]) for m in layers[1:]]
+        far = [tall] + [along(tall, layer) for layer in layers[1:]]
         tower = jnp.concatenate(far, axis=0)
         for mask in masks:
             value = swap(tower, mask) if mask else tower
-            both(0, None, [(mask, layer) for layer in layers], value)
+            both(0, [(mask, layer) for layer in layers], value)
     return pieces
 
 

time: 79.7 us -> 85.1 us (1.068)
  waiting for transfers between devices: 31.4 us -> 38.4 us
  starting transfers between devices: 27.7 us -> 26 us
    ppermute x24 -> x22, waiting for transfers between devices: 6.06 us -> 20.3 us  [swap(): return lax.ppermute(value, 'pair', [(p, p ^ mask) for p in range(n_pair)])]
    ppermute x8 -> x6, waiting for transfers between devices: 25.4 us -> 18.1 us  [along(): return lax.ppermute(value, 'tm', [(z, z ^ layer) for z in range(n_tm)])]
    ppermute x8 -> x6, starting transfers between devices: 11.1 us -> 9.92 us  [along(): return lax.ppermute(value, 'tm', [(z, z ^ layer) for z in range(n_tm)])]
    ppermute x24 -> x22, starting transfers between devices: 16.6 us -> 16.1 us  [swap(): return lax.ppermute(value, 'pair', [(p, p ^ mask) for p in range(n_pair)])]
  transfers between devices with their start and end apart: 32 -> 28, of which waited for: 8 -> 8; matrix products, arithmetic and copies ran while one was open for 0% -> 0% of each run, Pallas kernels for 22% -> 21%
where the time goes in v3:
time: 85.1 us; the launch traced here: 84.9 us
  waiting for transfers between devices  38.4 us (45%)
  starting transfers between devices  26 us (31%)
  Pallas kernels  19.1 us (22%)
  local copies, waits for them, and re-layouts  0.95 us (1%)
    ppermute x22, waiting for transfers between devices, swap(): return lax.ppermute(value, 'pair', [(p, p ^ mask) for p in range(n_pair)])  20.3 us
    ppermute x6, waiting for transfers between devices, along(): return lax.ppermute(value, 'tm', [(z, z ^ layer) for z in range(n_tm)])  18.1 us
    ppermute x22, starting transfers between devices, swap(): return lax.ppermute(value, 'pair', [(p, p ^ mask) for p in range(n_pair)])  16.1 us
    pallas_call x7, Pallas kernels, partial_rows(): pl.pallas_call(functools.partial(partial_kernel, masks, layers, first, ar...  10.2 us
    ppermute x6, starting transfers between devices, along(): return lax.ppermute(value, 'tm', [(z, z ^ layer) for z in range(n_tm)])  9.92 us
    pallas_call x1, Pallas kernels, first_rows(): pl.pallas_call(functools.partial(first_kernel, taus, coef, layers, masks,...  5.15 us
    pallas_call x1, Pallas kernels, screen(): pl.pallas_call(functools.partial(screen_kernel, [t[:2] for t in terms], l...  1.75 us
  transfers between devices with their start and end apart: 28, of which 8 were waited for; matrix products, arithmetic and copies ran while one was open for 0% of the time, Pallas kernels for 21%

profile of v3, /device:TPU:0, one launch (start us, length us, event | category | flops | bytes accessed | tf_op | source)
XLA Modules:
  0.0 84.9 jit_solution(5772567769642199081)
XLA Ops:
  0.0 0.9 %fusion = (bf16[48,768]{1,0:T(8,128)(2,1)S(1)}, bf16[48,768]{1,0:T(8,128)(2,1)S(1)}) fusion(bf16[48,1536]{1,0:T(8,128)(2,1)} %param.7), kind=kLoop, calls=%fused_computation.2 | loop fusion | bytes 294912 | tf_op jit(solution)/shard_map/slice | solution.py:360
  0.9 5.1 %collective-permute-start.18 = (bf16[48,768]{1,0:T(8,128)(2,1)S(1)}, bf16[48,768]{1,0:T(8,128)(2,1)S(1)}, u32[]{:S(2)}, u32[]{:S(2)}) collective-permute-start(bf16[48,768]{1,0:T(8,128)(2,1)S(1)} %get-tuple-element.15), channel_id=1, source_target_pairs={{0,3},{1,2},{2,1},{3,0},{4,7},{5,6},{6,5},{7,4},{8,11},{9,10},{10,... | collective-permute-start | bytes 221192 | tf_op jit(solution)/shard_map/ppermute | solution.py:341
  6.1 0.6 collective-permute-start.16
  6.7 2.6 %collective-permute-start.10 = (bf16[48,1536]{1,0:T(8,128)(2,1)}, bf16[48,1536]{1,0:T(8,128)(2,1)S(1)}, u32[]{:S(2)}, u32[]{:S(2)}) collective-permute-start(bf16[48,1536]{1,0:T(8,128)(2,1)} %param.7), channel_id=1, source_target_pairs={{0,24},{4,28},{8,16},{12,20},{16,8},{20,12},{24,0},{28,4},{1,25},{... | collective-permute-start | bytes 442376 | tf_op jit(solution)/shard_map/ppermute | solution.py:336
  9.8 0.8 collective-permute-start.8
  10.6 1.7 %collective-permute-done.17 = bf16[48,768]{1,0:T(8,128)(2,1)S(1)} collective-permute-done((bf16[48,768]{1,0:T(8,128)(2,1)S(1)}, bf16[48,768]{1,0:T(8,128)(2,1)S(1)}, u32[]{:S(2)}, u32[]{:S(2)}) %collective-permute-start.17) | collective-permute-done | bytes 73760 | tf_op jit(solution)/shard_map/ppermute | solution.py:341
  12.4 5.2 %first.1 = (f32[8,256]{1,0:T(8,128)S(1)}, bf16[1536,2048]{1,0:T(8,128)(2,1)S(1)}, bf16[384,768]{1,0:T(8,128)(2,1)S(1)}) custom-call(s32[8]{0:T(128)} %occ_block.1, s32[8]{0:T(128)} %vir_block.1, f32[1,256]{1,0:T(1,128)} %bitcast.3, f32[1,1024]{1,0:T(1,128)} %bitcast.2, bf16[1536,2048]{1,0:T(8,128)(2,1)} %source.1), custom_call_target="tpu_custom_call" | custom-call | flops 1207959552 | bytes 6291456 | tf_op jit(solution)/shard_map/first/pallas_call | solution.py:143
  18.0 1.4 %partial.12 = bf16[384,768]{1,0:T(8,128)(2,1)S(1)} custom-call(f32[8,256]{1,0:T(8,128)S(1)} %get-tuple-element.10.w_ref, bf16[1536,2048]{1,0:T(8,128)(2,1)S(1)} %get-tuple-element.11.held), custom_call_target="tpu_custom_call" | custom-call | flops 1207959552 | bytes 5898240 | tf_op jit(solution)/shard_map/partial/pallas_call | solution.py:188
  19.6 1.7 %collective-permute-start.20 = (bf16[192,768]{1,0:T(8,128)(2,1)S(1)}, bf16[192,768]{1,0:T(8,128)(2,1)S(1)}, u32[]{:S(2)}, u32[]{:S(2)}) collective-permute-start(bf16[192,768]{1,0:T(8,128)(2,1)S(1)} %pad_maximum_fusion.1.refs_6_.refs_2_), channel_id=1, source_target_pairs={{0,8},{4,12},{8,0},{12,4},{16,24},{20,28},{24,16},{28,20},{1,9},{5... | collective-permute-start | bytes 884744 | tf_op jit(solution)/shard_map/ppermute | solution.py:336
  21.4 1.5 %collective-permute-start.22 = (bf16[192,768]{1,0:T(8,128)(2,1)S(1)}, bf16[192,768]{1,0:T(8,128)(2,1)S(1)}, u32[]{:S(2)}, u32[]{:S(2)}) collective-permute-start(bf16[192,768]{1,0:T(8,128)(2,1)S(1)} %pad_maximum_fusion.1.refs_6_.refs_2_), channel_id=1, source_target_pairs={{0,16},{4,20},{8,24},{12,28},{16,0},{20,4},{24,8},{28,12},{1,17},{... | collective-permute-start | bytes 884744 | tf_op jit(solution)/shard_map/ppermute | solution.py:336
  23.1 1.4 %partial.7 = bf16[384,768]{1,0:T(8,128)(2,1)S(1)} custom-call(f32[8,256]{1,0:T(8,128)S(1)} %get-tuple-element.10.w_ref, bf16[1536,2048]{1,0:T(8,128)(2,1)S(1)} %get-tuple-element.11.held), custom_call_target="tpu_custom_call" | custom-call | flops 1207959552 | bytes 5898240 | tf_op jit(solution)/shard_map/partial/pallas_call | solution.py:188
  24.6 4.9 %collective-permute-done.20.refs_8_.refs_4_ = bf16[192,768]{1,0:T(8,128)(2,1)S(1)} collective-permute-done((bf16[192,768]{1,0:T(8,128)(2,1)S(1)}, bf16[192,768]{1,0:T(8,128)(2,1)S(1)}, u32[]{:S(2)}, u32[]{:S(2)}) %collective-permute-start.20) | collective-permute-done | bytes 294944 | tf_op jit(solution)/shard_map/ppermute | solution.py:336
  29.5 7.2 %collective-permute-done.22.refs_10_.refs_6_ = bf16[192,768]{1,0:T(8,128)(2,1)S(1)} collective-permute-done((bf16[192,768]{1,0:T(8,128)(2,1)S(1)}, bf16[192,768]{1,0:T(8,128)(2,1)S(1)}, u32[]{:S(2)}, u32[]{:S(2)}) %collective-permute-start.22) | collective-permute-done | bytes 294944 | tf_op jit(solution)/shard_map/ppermute | solution.py:336
  36.7 1.0 %collective-permute-start.12 = (bf16[192,768]{1,0:T(8,128)(2,1)S(1)}, bf16[192,768]{1,0:T(8,128)(2,1)S(1)}, u32[]{:S(2)}, u32[]{:S(2)}) collective-permute-start(bf16[192,768]{1,0:T(8,128)(2,1)S(1)} %pad_maximum_fusion.refs_0_), channel_id=1, source_target_pairs={{0,1},{1,0},{2,3},{3,2},{4,5},{5,4},{6,7},{7,6},{8,9},{9,8},{10,11... | collective-permute-start | bytes 884744 | tf_op jit(solution)/shard_map/ppermute | solution.py:341
  37.7 1.4 %partial.10 = bf16[384,768]{1,0:T(8,128)(2,1)S(1)} custom-call(f32[8,256]{1,0:T(8,128)S(1)} %get-tuple-element.10.w_ref, bf16[1536,2048]{1,0:T(8,128)(2,1)S(1)} %get-tuple-element.11.held), custom_call_target="tpu_custom_call" | custom-call | flops 1207959552 | bytes 5898240 | tf_op jit(solution)/shard_map/partial/pallas_call | solution.py:188
  39.3 1.9 %collective-permute-start.14 = (bf16[192,768]{1,0:T(8,128)(2,1)S(1)}, bf16[192,768]{1,0:T(8,128)(2,1)S(1)}, u32[]{:S(2)}, u32[]{:S(2)}) collective-permute-start(bf16[192,768]{1,0:T(8,128)(2,1)S(1)} %pad_maximum_fusion.refs_0_), channel_id=1, source_target_pairs={{0,2},{1,3},{2,0},{3,1},{4,6},{5,7},{6,4},{7,5},{8,10},{9,11},{10,... | collective-permute-start | bytes 884744 | tf_op jit(solution)/shard_map/ppermute | solution.py:341
  41.1 1.4 %partial.9 = bf16[384,768]{1,0:T(8,128)(2,1)S(1)} custom-call(f32[8,256]{1,0:T(8,128)S(1)} %get-tuple-element.10.w_ref, bf16[1536,2048]{1,0:T(8,128)(2,1)S(1)} %get-tuple-element.11.held, bf16[384,768]{1,0:T(8,128)(2,1)S(1)} %collective-permute-done.1.refs_0_), custom_call_target="tpu_custom_call" | custom-call | flops 1207959552 | bytes 5898240 | tf_op jit(solution)/shard_map/partial/pallas_call | solution.py:188
  42.8 1.4 %partial.13 = bf16[384,768]{1,0:T(8,128)(2,1)S(1)} custom-call(f32[8,256]{1,0:T(8,128)S(1)} %get-tuple-element.10.w_ref, bf16[1536,2048]{1,0:T(8,128)(2,1)S(1)} %get-tuple-element.11.held, bf16[384,768]{1,0:T(8,128)(2,1)S(1)} %collective-permute-done.5.refs_0_), custom_call_target="tpu_custom_call" | custom-call | flops 1207959552 | bytes 5898240 | tf_op jit(solution)/shard_map/partial/pallas_call | solution.py:188
  44.4 4.2 %collective-permute-start.6 = (bf16[384,768]{1,0:T(8,128)(2,1)S(1)}, bf16[384,768]{1,0:T(8,128)(2,1)S(1)}, u32[]{:S(2)}, u32[]{:S(2)}) collective-permute-start(bf16[384,768]{1,0:T(8,128)(2,1)S(1)} %partial.13), channel_id=1, source_target_pairs={{0,16},{4,20},{8,24},{12,28},{16,0},{20,4},{24,8},{28,12},{1,17},{... | collective-permute-start | bytes 1769480 | tf_op jit(solution)/shard_map/ppermute | solution.py:336
  48.6 7.3 %collective-permute-done.14.refs_4_ = bf16[192,768]{1,0:T(8,128)(2,1)S(1)} collective-permute-done((bf16[192,768]{1,0:T(8,128)(2,1)S(1)}, bf16[192,768]{1,0:T(8,128)(2,1)S(1)}, u32[]{:S(2)}, u32[]{:S(2)}) %collective-permute-start.14) | collective-permute-done | bytes 294944 | tf_op jit(solution)/shard_map/ppermute | solution.py:341
  55.9 1.3 %collective-permute-start.26 = (bf16[192,768]{1,0:T(8,128)(2,1)S(1)}, bf16[192,768]{1,0:T(8,128)(2,1)S(1)}, u32[]{:S(2)}, u32[]{:S(2)}) collective-permute-start(bf16[192,768]{1,0:T(8,128)(2,1)S(1)} %pad_maximum_fusion.refs_0_), channel_id=1, source_target_pairs={{0,3},{1,2},{2,1},{3,0},{4,7},{5,6},{6,5},{7,4},{8,11},{9,10},{10,... | collective-permute-start | bytes 884744 | tf_op jit(solution)/shard_map/ppermute | solution.py:341
  57.2 9.1 %collective-permute-done.26.refs_0_ = bf16[192,768]{1,0:T(8,128)(2,1)S(1)} collective-permute-done((bf16[192,768]{1,0:T(8,128)(2,1)S(1)}, bf16[192,768]{1,0:T(8,128)(2,1)S(1)}, u32[]{:S(2)}, u32[]{:S(2)}) %collective-permute-start.26) | collective-permute-done | bytes 294944 | tf_op jit(solution)/shard_map/ppermute | solution.py:341
  66.3 0.5 collective-permute-start.23
  66.9 1.4 %partial.8.mine.refs_0_ = f32[384,768]{1,0:T(8,128)S(1)} custom-call(f32[8,256]{1,0:T(8,128)S(1)} %get-tuple-element.10.w_ref, bf16[1536,2048]{1,0:T(8,128)(2,1)S(1)} %get-tuple-element.11.held, bf16[384,768]{1,0:T(8,128)(2,1)S(1)} %collective-permute-done.refs_0_), custom_call_target="tpu_custom_call" | custom-call | flops 1207959552 | bytes 5898240 | tf_op jit(solution)/shard_map/partial/pallas_call | solution.py:188
  68.3 0.5 collective-permute-start.13
  68.9 1.6 %partial.11.mine.refs_3_ = f32[384,768]{1,0:T(8,128)S(1)} custom-call(f32[8,256]{1,0:T(8,128)S(1)} %get-tuple-element.10.w_ref, bf16[1536,2048]{1,0:T(8,128)(2,1)S(1)} %get-tuple-element.11.held, bf16[384,768]{1,0:T(8,128)(2,1)S(1)} %collective-permute-done.4.refs_0_), custom_call_target="tpu_custom_call" | custom-call | flops 1207959552 | bytes 5898240 | tf_op jit(solution)/shard_map/partial/pallas_call | solution.py:188
  70.7 1.6 %collective-permute-start.3 = (bf16[192,768]{1,0:T(8,128)(2,1)S(1)}, bf16[192,768]{1,0:T(8,128)(2,1)S(1)}, u32[]{:S(2)}, u32[]{:S(2)}) collective-permute-start(bf16[192,768]{1,0:T(8,128)(2,1)S(1)} %pass_on.2), channel_id=1, source_target_pairs={{0,16},{4,20},{8,24},{12,28},{16,0},{20,4},{24,8},{28,12},{1,17},{... | collective-permute-start | bytes 884744 | tf_op jit(solution)/shard_map/ppermute | solution.py:336
  72.3 0.6 collective-permute-start.7
  73.2 6.9 %collective-permute-done.3.refs_2_ = bf16[192,768]{1,0:T(8,128)(2,1)S(1)} collective-permute-done((bf16[192,768]{1,0:T(8,128)(2,1)S(1)}, bf16[192,768]{1,0:T(8,128)(2,1)S(1)}, u32[]{:S(2)}, u32[]{:S(2)}) %collective-permute-start.3) | collective-permute-done | bytes 294944 | tf_op jit(solution)/shard_map/ppermute | solution.py:336
  80.1 1.3 %collective-permute-done.7.refs_5_ = bf16[192,768]{1,0:T(8,128)(2,1)S(1)} collective-permute-done((bf16[192,768]{1,0:T(8,128)(2,1)S(1)}, bf16[192,768]{1,0:T(8,128)(2,1)S(1)}, u32[]{:S(2)}, u32[]{:S(2)}) %collective-permute-start.7) | collective-permute-done | bytes 294944 | tf_op jit(solution)/shard_map/ppermute | solution.py:336
  81.4 1.7 %screen.1 = (f32[192,1536]{1,0:T(8,128)S(1)}, bf16[384,1536]{1,0:T(8,128)(2,1)S(1)}) custom-call(f32[384,768]{1,0:T(8,128)S(1)} %partial.8.mine.refs_0_, bf16[384,768]{1,0:T(8,128)(2,1)S(1)} %collective-permute-done.2.other.refs_1_, bf16[192,768]{1,0:T(8,128)(2,1)S(1)} %collective-permute-done.3.refs_2_, f32[384,768]{1,0:T(8,128)S(1)} %partial.11.mine.refs_3_, ...), custom_call_target="tpu_custom_call" | custom-call | flops 1358954496 | bytes 5308416 | tf_op jit(solution)/shard_map/screen/pallas_call | solution.py:279
  83.1 1.6 %finish.1 = f32[1,192,1536]{2,1,0:T(8,128)} custom-call(f32[192,1536]{1,0:T(8,128)S(1)} %get-tuple-element.13.total, bf16[384,1536]{1,0:T(8,128)(2,1)S(1)} %get-tuple-element.14.chi, bf16[192,768]{1,0:T(8,128)(2,1)S(1)} %collective-permute-done.26.refs_0_, bf16[192,768]{1,0:T(8,128)(2,1)S(1)} %collective-permute-done.27.refs_1_, ...), custom_call_target="tpu_custom_call" | custom-call | flops 226492416 | bytes 3538944 | tf_op jit(solution)/shard_map/finish/pallas_call | solution.py:316
  (43 shorter events, 2.6 us)
Async XLA Ops:
  0.9 8.9 %collective-permute-start.18 = (bf16[48,768]{1,0:T(8,128)(2,1)S(1)}, bf16[48,768]{1,0:T(8,128)(2,1)S(1)}, u32[]{:S(2)}, u32[]{:S(2)}) collective-permute-start(bf16[48,768]{1,0:T(8,128)(2,1)S(1)} %get-tuple-element.15), channel_id=1, source_target_pairs={{0,3},{1,2},{2,1},{3,0},{4,7},{5,6},{6,5},{7,4},{8,11},{9,10},{10,... | collective-permute-start | bytes 221192 | tf_op jit(solution)/shard_map/ppermute | solution.py:341
  6.1 6.2 %collective-permute-start.17 = (bf16[48,768]{1,0:T(8,128)(2,1)S(1)}, bf16[48,768]{1,0:T(8,128)(2,1)S(1)}, u32[]{:S(2)}, u32[]{:S(2)}) collective-permute-start(bf16[48,768]{1,0:T(8,128)(2,1)S(1)} %get-tuple-element.15), channel_id=1, source_target_pairs={{0,2},{1,3},{2,0},{3,1},{4,6},{5,7},{6,4},{7,5},{8,10},{9,11},{10,... | collective-permute-start | bytes 221192 | tf_op jit(solution)/shard_map/ppermute | solution.py:341
  6.1 6.2 %collective-permute-start.16 = (bf16[48,768]{1,0:T(8,128)(2,1)S(1)}, bf16[48,768]{1,0:T(8,128)(2,1)S(1)}, u32[]{:S(2)}, u32[]{:S(2)}) collective-permute-start(bf16[48,768]{1,0:T(8,128)(2,1)S(1)} %get-tuple-element.15), channel_id=1, source_target_pairs={{0,1},{1,0},{2,3},{3,2},{4,5},{5,4},{6,7},{7,6},{8,9},{9,8},{10,11... | collective-permute-start | bytes 221192 | tf_op jit(solution)/shard_map/ppermute | solution.py:341
  6.7 12.7 %collective-permute-start.10 = (bf16[48,1536]{1,0:T(8,128)(2,1)}, bf16[48,1536]{1,0:T(8,128)(2,1)S(1)}, u32[]{:S(2)}, u32[]{:S(2)}) collective-permute-start(bf16[48,1536]{1,0:T(8,128)(2,1)} %param.7), channel_id=1, source_target_pairs={{0,24},{4,28},{8,16},{12,20},{16,8},{20,12},{24,0},{28,4},{1,25},{... | collective-permute-start | bytes 442376 | tf_op jit(solution)/shard_map/ppermute | solution.py:336
  9.3 10.3 %collective-permute-start.9 = (bf16[48,1536]{1,0:T(8,128)(2,1)}, bf16[48,1536]{1,0:T(8,128)(2,1)S(1)}, u32[]{:S(2)}, u32[]{:S(2)}) collective-permute-start(bf16[48,1536]{1,0:T(8,128)(2,1)} %param.7), channel_id=1, source_target_pairs={{0,16},{4,20},{8,24},{12,28},{16,0},{20,4},{24,8},{28,12},{1,17},{... | collective-permute-start | bytes 442376 | tf_op jit(solution)/shard_map/ppermute | solution.py:336
  9.8 11.5 %collective-permute-start.8 = (bf16[48,1536]{1,0:T(8,128)(2,1)}, bf16[48,1536]{1,0:T(8,128)(2,1)S(1)}, u32[]{:S(2)}, u32[]{:S(2)}) collective-permute-start(bf16[48,1536]{1,0:T(8,128)(2,1)} %param.7), channel_id=1, source_target_pairs={{0,8},{4,12},{8,0},{12,4},{16,24},{20,28},{24,16},{28,20},{1,9},{5... | collective-permute-start | bytes 442376 | tf_op jit(solution)/shard_map/ppermute | solution.py:336
  12.3 10.6 %collective-permute-start.19 = (bf16[192,768]{1,0:T(8,128)(2,1)S(1)}, bf16[192,768]{1,0:T(8,128)(2,1)S(1)}, u32[]{:S(2)}, u32[]{:S(2)}) collective-permute-start(bf16[192,768]{1,0:T(8,128)(2,1)S(1)} %pad_maximum_fusion.1.refs_6_.refs_2_), channel_id=1, source_target_pairs={{0,4},{4,0},{8,12},{12,8},{16,20},{20,16},{24,28},{28,24},{1,5},{5... | collective-permute-start | bytes 884744 | tf_op jit(solution)/shard_map/ppermute | solution.py:336
  17.6 21.7 %collective-permute-start.1 = (bf16[384,768]{1,0:T(8,128)(2,1)S(1)}, bf16[384,768]{1,0:T(8,128)(2,1)S(1)}, u32[]{:S(2)}, u32[]{:S(2)}) collective-permute-start(bf16[384,768]{1,0:T(8,128)(2,1)S(1)} %get-tuple-element.12), channel_id=1, source_target_pairs={{0,4},{4,0},{8,12},{12,8},{16,20},{20,16},{24,28},{28,24},{1,5},{5... | collective-permute-start | bytes 1769480 | tf_op jit(solution)/shard_map/ppermute | solution.py:336
  19.5 23.1 %collective-permute-start.5 = (bf16[384,768]{1,0:T(8,128)(2,1)S(1)}, bf16[384,768]{1,0:T(8,128)(2,1)S(1)}, u32[]{:S(2)}, u32[]{:S(2)}) collective-permute-start(bf16[384,768]{1,0:T(8,128)(2,1)S(1)} %partial.12), channel_id=1, source_target_pairs={{0,4},{4,0},{8,12},{12,8},{16,20},{20,16},{24,28},{28,24},{1,5},{5... | collective-permute-start | bytes 1769480 | tf_op jit(solution)/shard_map/ppermute | solution.py:336
  19.6 9.9 %collective-permute-start.20 = (bf16[192,768]{1,0:T(8,128)(2,1)S(1)}, bf16[192,768]{1,0:T(8,128)(2,1)S(1)}, u32[]{:S(2)}, u32[]{:S(2)}) collective-permute-start(bf16[192,768]{1,0:T(8,128)(2,1)S(1)} %pad_maximum_fusion.1.refs_6_.refs_2_), channel_id=1, source_target_pairs={{0,8},{4,12},{8,0},{12,4},{16,24},{20,28},{24,16},{28,20},{1,9},{5... | collective-permute-start | bytes 884744 | tf_op jit(solution)/shard_map/ppermute | solution.py:336
  21.4 15.4 %collective-permute-start.22 = (bf16[192,768]{1,0:T(8,128)(2,1)S(1)}, bf16[192,768]{1,0:T(8,128)(2,1)S(1)}, u32[]{:S(2)}, u32[]{:S(2)}) collective-permute-start(bf16[192,768]{1,0:T(8,128)(2,1)S(1)} %pad_maximum_fusion.1.refs_6_.refs_2_), channel_id=1, source_target_pairs={{0,16},{4,20},{8,24},{12,28},{16,0},{20,4},{24,8},{28,12},{1,17},{... | collective-permute-start | bytes 884744 | tf_op jit(solution)/shard_map/ppermute | solution.py:336
  22.9 16.3 %collective-permute-start.24 = (bf16[192,768]{1,0:T(8,128)(2,1)S(1)}, bf16[192,768]{1,0:T(8,128)(2,1)S(1)}, u32[]{:S(2)}, u32[]{:S(2)}) collective-permute-start(bf16[192,768]{1,0:T(8,128)(2,1)S(1)} %pad_maximum_fusion.1.refs_6_.refs_2_), channel_id=1, source_target_pairs={{0,24},{4,28},{8,16},{12,20},{16,8},{20,12},{24,0},{28,4},{1,25},{... | collective-permute-start | bytes 884744 | tf_op jit(solution)/shard_map/ppermute | solution.py:336
  29.5 14.7 %collective-permute-start.11 = (bf16[192,768]{1,0:T(8,128)(2,1)S(1)}, bf16[192,768]{1,0:T(8,128)(2,1)S(1)}, u32[]{:S(2)}, u32[]{:S(2)}) collective-permute-start(bf16[192,768]{1,0:T(8,128)(2,1)S(1)} %pad_maximum_fusion.refs_0_), channel_id=1, source_target_pairs={{0,4},{4,0},{8,12},{12,8},{16,20},{20,16},{24,28},{28,24},{1,5},{5... | collective-permute-start | bytes 884744 | tf_op jit(solution)/shard_map/ppermute | solution.py:336
  36.7 7.7 %collective-permute-start.12 = (bf16[192,768]{1,0:T(8,128)(2,1)S(1)}, bf16[192,768]{1,0:T(8,128)(2,1)S(1)}, u32[]{:S(2)}, u32[]{:S(2)}) collective-permute-start(bf16[192,768]{1,0:T(8,128)(2,1)S(1)} %pad_maximum_fusion.refs_0_), channel_id=1, source_target_pairs={{0,1},{1,0},{2,3},{3,2},{4,5},{5,4},{6,7},{7,6},{8,9},{9,8},{10,11... | collective-permute-start | bytes 884744 | tf_op jit(solution)/shard_map/ppermute | solution.py:341
  39.2 27.1 %collective-permute-start = (bf16[384,768]{1,0:T(8,128)(2,1)S(1)}, bf16[384,768]{1,0:T(8,128)(2,1)S(1)}, u32[]{:S(2)}, u32[]{:S(2)}) collective-permute-start(bf16[384,768]{1,0:T(8,128)(2,1)S(1)} %partial.7), channel_id=1, source_target_pairs={{0,4},{4,0},{8,12},{12,8},{16,20},{20,16},{24,28},{28,24},{1,5},{5... | collective-permute-start | bytes 1769480 | tf_op jit(solution)/shard_map/ppermute | solution.py:336
  39.3 16.6 %collective-permute-start.14 = (bf16[192,768]{1,0:T(8,128)(2,1)S(1)}, bf16[192,768]{1,0:T(8,128)(2,1)S(1)}, u32[]{:S(2)}, u32[]{:S(2)}) collective-permute-start(bf16[192,768]{1,0:T(8,128)(2,1)S(1)} %pad_maximum_fusion.refs_0_), channel_id=1, source_target_pairs={{0,2},{1,3},{2,0},{3,1},{4,6},{5,7},{6,4},{7,5},{8,10},{9,11},{10,... | collective-permute-start | bytes 884744 | tf_op jit(solution)/shard_map/ppermute | solution.py:341
  42.6 24.2 %collective-permute-start.4 = (bf16[384,768]{1,0:T(8,128)(2,1)S(1)}, bf16[384,768]{1,0:T(8,128)(2,1)S(1)}, u32[]{:S(2)}, u32[]{:S(2)}) collective-permute-start(bf16[384,768]{1,0:T(8,128)(2,1)S(1)} %partial.10), channel_id=1, source_target_pairs={{0,4},{4,0},{8,12},{12,8},{16,20},{20,16},{24,28},{28,24},{1,5},{5... | collective-permute-start | bytes 1769480 | tf_op jit(solution)/shard_map/ppermute | solution.py:336
  44.2 24.1 %collective-permute-start.2 = (bf16[384,768]{1,0:T(8,128)(2,1)S(1)}, bf16[384,768]{1,0:T(8,128)(2,1)S(1)}, u32[]{:S(2)}, u32[]{:S(2)}) collective-permute-start(bf16[384,768]{1,0:T(8,128)(2,1)S(1)} %partial.9), channel_id=1, source_target_pairs={{0,8},{4,12},{8,0},{12,4},{16,24},{20,28},{24,16},{28,20},{1,9},{5... | collective-permute-start | bytes 1769480 | tf_op jit(solution)/shard_map/ppermute | solution.py:336
  44.4 24.4 %collective-permute-start.6 = (bf16[384,768]{1,0:T(8,128)(2,1)S(1)}, bf16[384,768]{1,0:T(8,128)(2,1)S(1)}, u32[]{:S(2)}, u32[]{:S(2)}) collective-permute-start(bf16[384,768]{1,0:T(8,128)(2,1)S(1)} %partial.13), channel_id=1, source_target_pairs={{0,16},{4,20},{8,24},{12,28},{16,0},{20,4},{24,8},{28,12},{1,17},{... | collective-permute-start | bytes 1769480 | tf_op jit(solution)/shard_map/ppermute | solution.py:336
  55.9 10.4 %collective-permute-start.26 = (bf16[192,768]{1,0:T(8,128)(2,1)S(1)}, bf16[192,768]{1,0:T(8,128)(2,1)S(1)}, u32[]{:S(2)}, u32[]{:S(2)}) collective-permute-start(bf16[192,768]{1,0:T(8,128)(2,1)S(1)} %pad_maximum_fusion.refs_0_), channel_id=1, source_target_pairs={{0,3},{1,2},{2,1},{3,0},{4,7},{5,6},{6,5},{7,4},{8,11},{9,10},{10,... | collective-permute-start | bytes 884744 | tf_op jit(solution)/shard_map/ppermute | solution.py:341
  66.3 4.4 %collective-permute-start.21 = (bf16[192,768]{1,0:T(8,128)(2,1)S(1)}, bf16[192,768]{1,0:T(8,128)(2,1)S(1)}, u32[]{:S(2)}, u32[]{:S(2)}) collective-permute-start(bf16[192,768]{1,0:T(8,128)(2,1)S(1)} %collective-permute-done.20.refs_8_.refs_4_), channel_id=1, source_target_pairs={{0,4},{4,0},{8,12},{12,8},{16,20},{20,16},{24,28},{28,24},{1,5},{5... | collective-permute-start | bytes 884744 | tf_op jit(solution)/shard_map/ppermute | solution.py:336
  66.3 6.0 %collective-permute-start.23 = (bf16[192,768]{1,0:T(8,128)(2,1)S(1)}, bf16[192,768]{1,0:T(8,128)(2,1)S(1)}, u32[]{:S(2)}, u32[]{:S(2)}) collective-permute-start(bf16[192,768]{1,0:T(8,128)(2,1)S(1)} %collective-permute-done.22.refs_10_.refs_6_), channel_id=1, source_target_pairs={{0,4},{4,0},{8,12},{12,8},{16,20},{20,16},{24,28},{28,24},{1,5},{5... | collective-permute-start | bytes 884744 | tf_op jit(solution)/shard_map/ppermute | solution.py:336
  66.8 6.1 %collective-permute-start.25 = (bf16[192,768]{1,0:T(8,128)(2,1)S(1)}, bf16[192,768]{1,0:T(8,128)(2,1)S(1)}, u32[]{:S(2)}, u32[]{:S(2)}) collective-permute-start(bf16[192,768]{1,0:T(8,128)(2,1)S(1)} %collective-permute-done.24.refs_12_.refs_8_), channel_id=1, source_target_pairs={{0,4},{4,0},{8,12},{12,8},{16,20},{20,16},{24,28},{28,24},{1,5},{5... | collective-permute-start | bytes 884744 | tf_op jit(solution)/shard_map/ppermute | solution.py:336
  68.3 4.6 %collective-permute-start.13 = (bf16[192,768]{1,0:T(8,128)(2,1)S(1)}, bf16[192,768]{1,0:T(8,128)(2,1)S(1)}, u32[]{:S(2)}, u32[]{:S(2)}) collective-permute-start(bf16[192,768]{1,0:T(8,128)(2,1)S(1)} %collective-permute-done.12.refs_2_), channel_id=1, source_target_pairs={{0,4},{4,0},{8,12},{12,8},{16,20},{20,16},{24,28},{28,24},{1,5},{5... | collective-permute-start | bytes 884744 | tf_op jit(solution)/shard_map/ppermute | solution.py:336
  68.8 4.1 %collective-permute-start.15 = (bf16[192,768]{1,0:T(8,128)(2,1)S(1)}, bf16[192,768]{1,0:T(8,128)(2,1)S(1)}, u32[]{:S(2)}, u32[]{:S(2)}) collective-permute-start(bf16[192,768]{1,0:T(8,128)(2,1)S(1)} %collective-permute-done.14.refs_4_), channel_id=1, source_target_pairs={{0,4},{4,0},{8,12},{12,8},{16,20},{20,16},{24,28},{28,24},{1,5},{5... | collective-permute-start | bytes 884744 | tf_op jit(solution)/shard_map/ppermute | solution.py:336
  70.7 9.4 %collective-permute-start.3 = (bf16[192,768]{1,0:T(8,128)(2,1)S(1)}, bf16[192,768]{1,0:T(8,128)(2,1)S(1)}, u32[]{:S(2)}, u32[]{:S(2)}) collective-permute-start(bf16[192,768]{1,0:T(8,128)(2,1)S(1)} %pass_on.2), channel_id=1, source_target_pairs={{0,16},{4,20},{8,24},{12,28},{16,0},{20,4},{24,8},{28,12},{1,17},{... | collective-permute-start | bytes 884744 | tf_op jit(solution)/shard_map/ppermute | solution.py:336
  72.3 9.1 %collective-permute-start.7 = (bf16[192,768]{1,0:T(8,128)(2,1)S(1)}, bf16[192,768]{1,0:T(8,128)(2,1)S(1)}, u32[]{:S(2)}, u32[]{:S(2)}) collective-permute-start(bf16[192,768]{1,0:T(8,128)(2,1)S(1)} %pass_on.3), channel_id=1, source_target_pairs={{0,8},{4,12},{8,0},{12,4},{16,24},{20,28},{24,16},{28,20},{1,9},{5... | collective-permute-start | bytes 884744 | tf_op jit(solution)/shard_map/ppermute | solution.py:336
  72.9 10.2 %collective-permute-start.27 = (bf16[192,768]{1,0:T(8,128)(2,1)S(1)}, bf16[192,768]{1,0:T(8,128)(2,1)S(1)}, u32[]{:S(2)}, u32[]{:S(2)}) collective-permute-start(bf16[192,768]{1,0:T(8,128)(2,1)S(1)} %collective-permute-done.26.refs_0_), channel_id=1, source_target_pairs={{0,4},{4,0},{8,12},{12,8},{16,20},{20,16},{24,28},{28,24},{1,5},{5... | collective-permute-start | bytes 884744 | tf_op jit(solution)/shard_map/ppermute | solution.py:336
